TPU v7x, 8 devices: a whole 2x2x1 slice. The times are simulated.
8 devices in a mesh: dp: 2 (over z, y), tp: 4 (over x, core).
Axes of the slice: x: 2, y: 2, z: 1, core: 2. Of those that a mesh axis runs over, the one named last changes fastest.
Arguments:
- tokens: int32 [64, 256], P('dp'), parts along dimension 0
- attn_mask: int32 [64, 256], P('dp'), parts along dimension 0
- emb_table: bfloat16 [50272, 768], P('tp')
- pos_table: bfloat16 [2050, 768], replicated
- ln1_gain: bfloat16 [768], replicated
- ln1_shift: bfloat16 [768], replicated
- w_qkv: bfloat16 [3, 768, 12, 64], P(None, None, 'tp')
- b_qkv: bfloat16 [3, 12, 64], P(None, 'tp')
- w_out: bfloat16 [12, 64, 768], P('tp')
- b_out: bfloat16 [768], replicated
- ln2_gain: bfloat16 [768], replicated
- ln2_shift: bfloat16 [768], replicated
- w_fc1: bfloat16 [768, 3072], P(None, 'tp')
- b_fc1: bfloat16 [3072], P('tp')
- w_fc2: bfloat16 [3072, 768], P('tp')
- b_fc2: bfloat16 [768], replicated
- grad_y: bfloat16 [64, 256, 768], P('dp', 'tp'), parts along dimension 0
Outputs:
- output 1: bfloat16 [64, 256, 768], P('dp', 'tp'), parts along dimension 0
- output 2: float32 [100544, 768], P(('dp', 'tp')), parts along dimension 0
- output 3: float32 [4100, 768], P('dp'), parts along dimension 0
- output 4: float32 [1536], P('dp'), parts along dimension 0
- output 5: float32 [1536], P('dp'), parts along dimension 0
- output 6: float32 [6, 768, 12, 64], P('dp', None, 'tp'), parts along dimension 0
- output 7: float32 [6, 12, 64], P('dp', 'tp'), parts along dimension 0
- output 8: float32 [24, 64, 768], P(('dp', 'tp')), parts along dimension 0
- output 9: float32 [1536], P('dp'), parts along dimension 0
- output 10: float32 [1536], P('dp'), parts along dimension 0
- output 11: float32 [1536], P('dp'), parts along dimension 0
- output 12: float32 [1536, 3072], P('dp', 'tp'), parts along dimension 0
- output 13: float32 [6144], P(('dp', 'tp')), parts along dimension 0
- output 14: float32 [6144, 768], P(('dp', 'tp')), parts along dimension 0
- output 15: float32 [1536], P('dp'), parts along dimension 0
There are 2 independent parts. A program takes and returns all parts, laid end to end along the dimension named above; an argument that names none is the same for every part.
All inputs are finite; a program needn't handle non-finite values.
Results may differ from a plain program's by a relative error of at most 0.02.
Values are sent between devices in bfloat16 or wider.
A program may use at most 1 GiB of HBM per device.

v0:
```python
import math
import jax
import jax.numpy as jnp
from jax import lax
from jax.sharding import PartitionSpec as P

LN_EPS = 1e-5
NEG_BIG = -1e30


def layer_norm(hidden, ln_gain, ln_shift):
    hidden32 = hidden.astype(jnp.float32)
    centered = hidden32 - jnp.mean(hidden32, axis=-1, keepdims=True)
    variance = jnp.mean(jnp.square(centered), axis=-1, keepdims=True)
    scaled = centered * lax.rsqrt(variance + LN_EPS)
    return (scaled * ln_gain + ln_shift).astype(jnp.bfloat16)


def layer_pass(hidden0, attn_mask, grad_y, ln1_gain, ln1_shift, w_qkv, b_qkv, w_out, b_out, ln2_gain, ln2_shift, w_fc1, b_fc1, w_fc2, b_fc2):
    seq_len = attn_mask.shape[1]
    q_scale = 1.0 / math.sqrt(w_qkv.shape[3])
    seq_index = jnp.arange(seq_len)
    causal = (seq_index[:, None] >= seq_index[None, :])[None, None]
    diagonal = (seq_index[:, None] == seq_index[None, :])[None, None]
    allowed = causal & ((attn_mask[:, None, None, :] == 1) | diagonal)
    normed1, norm1_pull = jax.vjp(layer_norm, hidden0, ln1_gain.astype(jnp.float32), ln1_shift.astype(jnp.float32))
    normed1_full = lax.all_gather(normed1, 'tp', axis=1, tiled=True)
    qkv_proj = jnp.einsum('bsd,tdhe->tbshe', normed1_full, w_qkv, preferred_element_type=jnp.float32) + b_qkv.astype(jnp.float32)[:, None, None]
    query_rows = (qkv_proj[0] * q_scale).astype(jnp.bfloat16)
    key_rows = qkv_proj[1].astype(jnp.bfloat16)
    value_rows = qkv_proj[2].astype(jnp.bfloat16)
    scores = jnp.einsum('bqhe,bkhe->bhqk', query_rows, key_rows, preferred_element_type=jnp.float32)
    attn_probs = jax.nn.softmax(jnp.where(allowed, scores, NEG_BIG), axis=-1)
    probs_low = attn_probs.astype(jnp.bfloat16)
    context = jnp.einsum('bhqk,bkhe->bqhe', probs_low, value_rows, preferred_element_type=jnp.float32).astype(jnp.bfloat16)
    attn_part = jnp.einsum('crif,ife->cre', context, w_out, preferred_element_type=jnp.float32).astype(jnp.bfloat16)
    attn_rows = lax.psum_scatter(attn_part, 'tp', scatter_dimension=1, tiled=True)
    hidden1 = (hidden0.astype(jnp.float32) + attn_rows.astype(jnp.float32) + b_out.astype(jnp.float32)).astype(jnp.bfloat16)
    normed2, norm2_pull = jax.vjp(layer_norm, hidden1, ln2_gain.astype(jnp.float32), ln2_shift.astype(jnp.float32))
    normed2_full = lax.all_gather(normed2, 'tp', axis=1, tiled=True)
    mlp_inner = jax.nn.relu(jnp.einsum('bsd,df->bsf', normed2_full, w_fc1, preferred_element_type=jnp.float32) + b_fc1.astype(jnp.float32)).astype(jnp.bfloat16)
    mlp_part = jnp.einsum('bsf,fd->bsd', mlp_inner, w_fc2, preferred_element_type=jnp.float32).astype(jnp.bfloat16)
    mlp_rows = lax.psum_scatter(mlp_part, 'tp', scatter_dimension=1, tiled=True)
    out_rows = (hidden1.astype(jnp.float32) + mlp_rows.astype(jnp.float32) + b_fc2.astype(jnp.float32)).astype(jnp.bfloat16)

    grad_full = lax.all_gather(grad_y, 'tp', axis=1, tiled=True)
    d_w_fc2 = jnp.einsum('bsf,bsd->fd', mlp_inner, grad_full, preferred_element_type=jnp.float32)
    d_inner = jnp.einsum('bsd,fd->bsf', grad_full, w_fc2, preferred_element_type=jnp.float32)
    d_pre1 = jnp.where(mlp_inner > 0, d_inner, 0.0)
    d_b_fc1 = jnp.sum(d_pre1, axis=(0, 1))
    d_pre1_low = d_pre1.astype(jnp.bfloat16)
    d_w_fc1 = jnp.einsum('bsd,bsf->df', normed2_full, d_pre1_low, preferred_element_type=jnp.float32)
    d_norm2_part = jnp.einsum('bsf,df->bsd', d_pre1_low, w_fc1, preferred_element_type=jnp.float32).astype(jnp.bfloat16)
    d_norm2 = lax.psum_scatter(d_norm2_part, 'tp', scatter_dimension=1, tiled=True)
    d_hidden1_ln, d_ln2_gain, d_ln2_shift = norm2_pull(d_norm2)
    d_hidden1 = (grad_y.astype(jnp.float32) + d_hidden1_ln.astype(jnp.float32)).astype(jnp.bfloat16)
    d_hidden1_full = lax.all_gather(d_hidden1, 'tp', axis=1, tiled=True)
    d_w_out = jnp.einsum('crif,cre->ife', context, d_hidden1_full, preferred_element_type=jnp.float32)
    d_context = jnp.einsum('cre,ife->crif', d_hidden1_full, w_out, preferred_element_type=jnp.float32).astype(jnp.bfloat16)
    d_value = jnp.einsum('bhqk,bqhe->bkhe', probs_low, d_context, preferred_element_type=jnp.float32)
    d_probs = jnp.einsum('bqhe,bkhe->bhqk', d_context, value_rows, preferred_element_type=jnp.float32)
    d_scores = (attn_probs * (d_probs - jnp.sum(d_probs * attn_probs, axis=-1, keepdims=True))).astype(jnp.bfloat16)
    d_query = jnp.einsum('bhqk,bkhe->bqhe', d_scores, key_rows, preferred_element_type=jnp.float32) * q_scale
    d_key = jnp.einsum('bhqk,bqhe->bkhe', d_scores, query_rows, preferred_element_type=jnp.float32)
    d_qkv = jnp.stack([d_query, d_key, d_value])
    d_b_qkv = jnp.sum(d_qkv, axis=(1, 2))
    d_qkv_low = d_qkv.astype(jnp.bfloat16)
    d_w_qkv = jnp.einsum('bsd,tbshe->tdhe', normed1_full, d_qkv_low, preferred_element_type=jnp.float32)
    d_norm1_part = jnp.einsum('tbshe,tdhe->bsd', d_qkv_low, w_qkv, preferred_element_type=jnp.float32).astype(jnp.bfloat16)
    d_norm1 = lax.psum_scatter(d_norm1_part, 'tp', scatter_dimension=1, tiled=True)
    d_hidden0_ln, d_ln1_gain, d_ln1_shift = norm1_pull(d_norm1)
    d_hidden0 = d_hidden1.astype(jnp.float32) + d_hidden0_ln.astype(jnp.float32)
    small_sums = lax.psum((d_ln1_gain, d_ln1_shift, jnp.sum(d_hidden1.astype(jnp.float32), axis=(0, 1)), d_ln2_gain, d_ln2_shift, jnp.sum(grad_y.astype(jnp.float32), axis=(0, 1))), 'tp')
    layer_grads = (small_sums[0], small_sums[1], d_w_qkv, d_b_qkv, d_w_out, small_sums[2], small_sums[3], small_sums[4], d_w_fc1, d_b_fc1, d_w_fc2, small_sums[5])
    return out_rows, d_hidden0, layer_grads


def solution(mesh):
    def device_step(tokens, attn_mask, emb_local, pos_table, ln1_gain, ln1_shift, w_qkv, b_qkv, w_out, b_out, ln2_gain, ln2_shift, w_fc1, b_fc1, w_fc2, b_fc2, grad_y):
        vocab_local, d_model = emb_local.shape
        seq_local = grad_y.shape[1]
        tp_rank = lax.axis_index('tp')
        local_ids = tokens - tp_rank * vocab_local
        is_owned = (local_ids >= 0) & (local_ids < vocab_local)
        emb_part = jnp.where(is_owned[:, :, None], jnp.take(emb_local, jnp.where(is_owned, local_ids, 0), axis=0), jnp.zeros((), jnp.bfloat16))
        emb_rows = lax.psum_scatter(emb_part, 'tp', scatter_dimension=1, tiled=True)
        positions = jnp.cumsum(attn_mask, axis=1) * attn_mask + 1
        pos_local = lax.dynamic_slice_in_dim(positions, tp_rank * seq_local, seq_local, axis=1)
        hidden0 = (emb_rows.astype(jnp.float32) + jnp.take(pos_table, pos_local, axis=0).astype(jnp.float32)).astype(jnp.bfloat16)
        out_rows, d_hidden0, layer_grads = layer_pass(hidden0, attn_mask, grad_y, ln1_gain, ln1_shift, w_qkv, b_qkv, w_out, b_out, ln2_gain, ln2_shift, w_fc1, b_fc1, w_fc2, b_fc2)
        d_pos = lax.psum(jax.ops.segment_sum(d_hidden0.reshape(-1, d_model), pos_local.reshape(-1), num_segments=pos_table.shape[0]), 'tp')
        d_hidden0_full = lax.all_gather(d_hidden0.astype(jnp.bfloat16), 'tp', axis=1, tiled=True)
        owner_ids = jnp.where(is_owned, local_ids, vocab_local)
        d_emb = jax.ops.segment_sum(d_hidden0_full.astype(jnp.float32).reshape(-1, d_model), owner_ids.reshape(-1), num_segments=vocab_local)
        return (out_rows, d_emb, d_pos) + layer_grads

    in_specs = (P('dp', None), P('dp', None), P('tp', None), P(None, None), P(None), P(None), P(None, None, 'tp', None), P(None, 'tp', None), P('tp', None, None), P(None), P(None), P(None), P(None, 'tp'), P('tp'), P('tp', None), P(None), P('dp', 'tp', None))
    out_specs = (P('dp', 'tp', None), P(('dp', 'tp'), None), P('dp', None), P('dp'), P('dp'), P('dp', None, 'tp', None), P('dp', 'tp', None), P(('dp', 'tp'), None, None), P('dp'), P('dp'), P('dp'), P('dp', 'tp'), P(('dp', 'tp')), P(('dp', 'tp'), None), P('dp'))
    return jax.shard_map(device_step, mesh=mesh, in_specs=in_specs, out_specs=out_specs, check_vma=False)
```

profile of v0, /device:TPU:0, one launch (start us, length us, event | category | flops | bytes accessed | tf_op | source)
XLA Modules:
  0.0 1327.3 jit_solution(12420597816619250860)
XLA Ops:
  9.6 46.0 %gather_fusion = bf16[8192,768]{1,0:T(8,128)(2,1)} fusion(bf16[12568,768]{1,0:T(8,128)(2,1)} %param.19, s32[8192]{0:T(1024)S(1)} %broadcast_clamp_fusion), kind=kCustom, calls=%fused_computation | custom fusion | bytes 25198592 | tf_op jit(solution)/shard_map/jit(_take)/gather | solution.py:85
  77.5 81.7 %reduce-scatter.6.cloned.1.call-done = bf16[32,64,768]{2,1,0:T(8,128)(2,1)} async-done(((bf16[32,256,768]{2,1,0:T(8,128)(2,1)}), bf16[32,64,768]{2,1,0:T(8,128)(2,1)}) %reduce-scatter.6.cloned.1.call-update) | async-done | bytes 3145744 | tf_op jit(solution)/shard_map/reduce_scatter | solution.py:86
  170.9 76.9 %all-gather.6.cloned.1.call-done = bf16[32,256,768]{2,1,0:T(8,128)(2,1)} async-done(((bf16[32,64,768]{2,1,0:T(8,128)(2,1)}), bf16[32,256,768]{2,1,0:T(8,128)(2,1)}) %all-gather.6.cloned.1.call-update) | async-done | bytes 12582928 | tf_op jit(solution)/shard_map/all_gather | solution.py:27
  247.8 16.2 %fusion.115 = (bf16[3,32,256,3,64]{2,4,3,0,1:T(8,128)(2,1)}, f32[3,32,256,3,64]{2,4,3,0,1:T(8,128)}) fusion(f32[3,3,64]{2,1,0:T(4,128)S(1)} %convert_element_type.149, bf16[3,768,3,64]{1,3,2,0:T(8,128)(2,1)} %param.23, bf16[32,256,768]{2,1,0:T(8,128)(2,1)} %all-gather.6.cloned.1.call-done), kind=kOutput, calls=%fused_computation.160 | convolution fusion | flops 7257194496 | bytes 41781504 | tf_op jit(solution)/shard_map/bsd,tdhe->tbshe/dot_general | solution.py:28
  264.0 16.1 %fusion.67 = f32[32,3,256,256]{2,3,1,0:T(8,128)} fusion(bf16[3,32,256,3,64]{2,4,3,0,1:T(8,128)(2,1)} %get-tuple-element.45, f32[3,32,256,3,64]{2,4,3,0,1:T(8,128)} %get-tuple-element.46), kind=kOutput, calls=%fused_computation.106 | convolution fusion | flops 808452096 | bytes 34603008 | tf_op jit(solution)/shard_map/bqhe,bkhe->bhqk/dot_general | solution.py:32
  280.1 34.7 %fusion.116 = (f32[32,3,256]{2,1,0:T(4,128)S(1)}, f32[32,3,256,256]{2,3,1,0:T(8,128)}) fusion(f32[32,3,256,256]{2,3,1,0:T(8,128)} %fusion.67, pred[32,256,256]{1,2,0:T(8,128)(4,1)} %or_and_fusion), kind=kOutput, calls=%fused_computation.161 | output fusion | flops 25166080 | bytes 52527104 | tf_op jit(solution)/shard_map/sub | solution.py:33
  314.8 13.2 fusion.71
  338.9 90.0 %reduce-scatter.8.cloned.1.call-done = bf16[32,64,768]{2,1,0:T(8,128)(2,1)} async-done(((bf16[32,256,768]{2,1,0:T(8,128)(2,1)}), bf16[32,64,768]{2,1,0:T(8,128)(2,1)}) %reduce-scatter.8.cloned.1.call-update) | async-done | bytes 3145744 | tf_op jit(solution)/shard_map/reduce_scatter | solution.py:37
  436.8 79.5 %all-gather.8.cloned.1.call-done = bf16[32,256,768]{2,1,0:T(8,128)(2,1)} async-done(((bf16[32,64,768]{2,1,0:T(8,128)(2,1)}), bf16[32,256,768]{2,1,0:T(8,128)(2,1)}) %all-gather.8.cloned.1.call-update) | async-done | bytes 12582928 | tf_op jit(solution)/shard_map/all_gather | solution.py:40
  516.3 17.9 %convert_reduce_fusion = (u32[256,768]{1,0:T(8,128)S(1)}, bf16[32,256,768]{2,1,0:T(8,128)(2,1)}) fusion(f32[768]{0:T(1024)S(1)} %convert_element_type.165, bf16[32,256,768]{2,1,0:T(8,128)(2,1)} %all-gather.8.cloned.1.call-done, bf16[768,768]{1,0:T(8,128)(2,1)S(1)} %copy-done.35), kind=kOutput, calls=%fused_computation.6 | convolution fusion | flops 9720102912 | bytes 27134976 | tf_op jit(solution)/shard_map/bsd,df->bsf/dot_general | solution.py:41
  534.2 63.5 %all-gather.10.cloned.1.call-done = bf16[32,256,768]{2,1,0:T(8,128)(2,1)} async-done(((bf16[32,64,768]{2,1,0:T(8,128)(2,1)}), bf16[32,256,768]{2,1,0:T(8,128)(2,1)}) %all-gather.10.cloned.1.call-update) | async-done | bytes 12582928 | tf_op jit(solution)/shard_map/all_gather | solution.py:46
  597.7 18.0 %fusion.5 = (f32[768]{0:T(1024)}, bf16[32,256,768]{2,1,0:T(8,128)(2,1)}) fusion(u32[256,768]{1,0:T(8,128)S(1)} %get-tuple-element.49, bf16[32,256,768]{2,1,0:T(8,128)(2,1)} %all-gather.10.cloned.1.call-done, bf16[768,768]{1,0:T(8,128)(2,1)S(1)} %copy-done.36), kind=kOutput, calls=%fused_computation.18 | convolution fusion | flops 9701424128 | bytes 27134976 | tf_op jit(solution)/shard_map/bsd,fd->bsf/dot_general | solution.py:48
  615.7 17.1 %convolution_convert_fusion = bf16[32,256,768]{2,1,0:T(8,128)(2,1)} fusion(bf16[32,256,768]{2,1,0:T(8,128)(2,1)} %get-tuple-element.54, u32[256,768]{1,0:T(8,128)S(1)} %get-tuple-element.49, bf16[768,768]{1,0:T(8,128)(2,1)S(1)} %copy-done.35), kind=kOutput, calls=%fused_computation.66 | convolution fusion | flops 9695133696 | bytes 27131904 | tf_op jit(solution)/shard_map/bsf,df->bsd/dot_general | solution.py:53
  632.8 17.3 %convolution_convert_fusion.1 = bf16[32,256,768]{2,1,0:T(8,128)(2,1)} fusion(bf16[32,256,768]{2,1,0:T(8,128)(2,1)} %get-tuple-element.50, bf16[768,768]{1,0:T(8,128)(2,1)S(1)} %copy-done.36), kind=kOutput, calls=%fused_computation.67 | convolution fusion | flops 9669967872 | bytes 26345472 | tf_op jit(solution)/shard_map/bsf,fd->bsd/dot_general | solution.py:42
  650.8 72.7 %reduce-scatter.12.cloned.1.call-done = bf16[32,64,768]{2,1,0:T(8,128)(2,1)} async-done(((bf16[32,256,768]{2,1,0:T(8,128)(2,1)}), bf16[32,64,768]{2,1,0:T(8,128)(2,1)}) %reduce-scatter.12.cloned.1.call-update) | async-done | bytes 3145744 | tf_op jit(solution)/shard_map/reduce_scatter | solution.py:54
  732.7 84.0 %reduce-scatter.10.cloned.1.call-done = bf16[32,64,768]{2,1,0:T(8,128)(2,1)} async-done(((bf16[32,256,768]{2,1,0:T(8,128)(2,1)}), bf16[32,64,768]{2,1,0:T(8,128)(2,1)}) %reduce-scatter.10.cloned.1.call-update) | async-done | bytes 3145744 | tf_op jit(solution)/shard_map/reduce_scatter | solution.py:43
  825.0 80.1 %all-gather.12.cloned.1.call-done = bf16[32,256,768]{2,1,0:T(8,128)(2,1)} async-done(((bf16[32,64,768]{2,1,0:T(8,128)(2,1)}), bf16[32,256,768]{2,1,0:T(8,128)(2,1)}) %all-gather.12.cloned.1.call-update) | async-done | bytes 12582928 | tf_op jit(solution)/shard_map/all_gather | solution.py:57
  905.1 10.5 fusion.74
  915.5 14.2 %fusion.68 = f32[1,32,256,3,64]{2,4,3,1,0:T(8,128)} fusion(bf16[32,256,3,64]{1,3,2,0:T(8,128)(2,1)} %fusion.74, f32[32,3,256,256]{2,3,1,0:T(8,128)} %get-tuple-element.48, f32[32,3,256]{2,1,0:T(4,128)S(1)} %copy-done.12), kind=kOutput, calls=%fused_computation.107 | convolution fusion | flops 817889280 | bytes 34701312 | tf_op jit(solution)/shard_map/bhqk,bqhe->bkhe/dot_general | solution.py:60
  929.7 21.1 %multiply_reduce_fusion = (f32[32,3,256]{2,1,0:T(4,128)S(1)}, f32[32,3,256,256]{2,3,1,0:T(8,128)}) fusion(f32[32,3,256,256]{2,3,1,0:T(8,128)} %get-tuple-element.48, f32[32,3,256]{2,1,0:T(4,128)S(1)} %copy-done.12, bf16[32,256,3,64]{1,3,2,0:T(8,128)(2,1)} %fusion.74, bf16[3,32,256,3,64]{2,4,3,0,1:T(8,128)(2,1)} %get-tuple-element.45), kind=kOutput, calls=%fused_computation.12 | convolution fusion | flops 824156160 | bytes 56819712 | tf_op jit(solution)/shard_map/bqhe,bkhe->bhqk/dot_general | solution.py:61
  950.8 21.4 %multiply_convert_fusion = bf16[32,3,256,256]{2,3,1,0:T(8,128)(2,1)} fusion(f32[32,3,256,256]{2,3,1,0:T(8,128)} %get-tuple-element.52, f32[32,3,256]{2,1,0:T(4,128)S(1)} %get-tuple-element.51, f32[32,3,256,256]{2,3,1,0:T(8,128)} %get-tuple-element.48, f32[32,3,256]{2,1,0:T(4,128)S(1)} %copy-done.12), kind=kLoop, calls=%fused_computation.11 | loop fusion | flops 25165824 | bytes 63111168 | tf_op jit(solution)/shard_map/convert_element_type | solution.py:62
  972.2 12.9 convolution_bitcast_fusion
  985.1 10.5 multiply_bitcast_fusion
  995.6 16.9 %bitcast_convert_fusion = bf16[32,256,768]{2,1,0:T(8,128)(2,1)} fusion(bf16[3,768,3,64]{1,3,2,0:T(8,128)(2,1)S(1)} %copy-done.37, f32[1,32,256,3,64]{2,4,3,1,0:T(8,128)} %fusion.68, f32[1,32,256,3,64]{2,4,3,1,0:T(8,128)} %convolution_bitcast_fusion, f32[1,32,256,3,64]{2,4,3,1,0:T(8,128)} %multiply_bitcast_fusion), kind=kOutput, calls=%fused_computation.9 | convolution fusion | flops 7263485952 | bytes 32342016 | tf_op jit(solution)/shard_map/tbshe,tdhe->bsd/dot_general | solution.py:69
  1012.6 90.6 %reduce-scatter.14.cloned.1.call-done = bf16[32,64,768]{2,1,0:T(8,128)(2,1)} async-done(((bf16[32,256,768]{2,1,0:T(8,128)(2,1)}), bf16[32,64,768]{2,1,0:T(8,128)(2,1)}) %reduce-scatter.14.cloned.1.call-update) | async-done | bytes 3145744 | tf_op jit(solution)/shard_map/reduce_scatter | solution.py:70
  1116.8 16.5 %convolution_bitcast_fusion.1 = f32[768,768]{1,0:T(8,128)} fusion(bf16[32,256,768]{2,1,0:T(8,128)(2,1)} %get-tuple-element.50, bf16[32,256,768]{2,1,0:T(8,128)(2,1)} %all-gather.10.cloned.1.call-done), kind=kOutput, calls=%fused_computation.111 | convolution fusion | flops 9663676416 | bytes 27525120 | tf_op jit(solution)/shard_map/bsf,bsd->fd/dot_general | solution.py:47
  1133.3 17.1 %convolution_bitcast_fusion.2 = f32[768,768]{1,0:T(8,128)} fusion(bf16[32,256,768]{2,1,0:T(8,128)(2,1)} %all-gather.8.cloned.1.call-done, bf16[32,256,768]{2,1,0:T(8,128)(2,1)} %get-tuple-element.54, u32[256,768]{1,0:T(8,128)S(1)} %copy-done.41), kind=kOutput, calls=%fused_computation.112 | convolution fusion | flops 9688842240 | bytes 28311552 | tf_op jit(solution)/shard_map/bsd,bsf->df/dot_general | solution.py:52
  1150.5 18.6 %scatter_custom_fusion.1 = f32[2050,768]{1,0:T(8,128)} fusion(s32[2048]{0:T(1024)S(1)} %reshape.205, f32[2048,768]{1,0:T(8,128)} %bitcast.150, f32[]{:T(128)} %constant.74.clone.1), kind=kCustom, calls=%fused_computation.97 | custom fusion | flops 1572864 | bytes 6298112 | tf_op jit(solution)/shard_map/scatter-add | solution.py:91
  1185.3 16.0 %fusion.77 = f32[3,768,3,64]{1,3,2,0:T(8,128)} fusion(bf16[32,256,768]{2,1,0:T(8,128)(2,1)} %all-gather.6.cloned.1.call-done, f32[1,32,256,3,64]{2,4,3,1,0:T(8,128)} %fusion.68, f32[1,32,256,3,64]{2,4,3,1,0:T(8,128)} %convolution_bitcast_fusion, f32[1,32,256,3,64]{2,4,3,1,0:T(8,128)} %multiply_bitcast_fusion), kind=kOutput, calls=%fused_computation.113 | convolution fusion | flops 7257194496 | bytes 33226752 | tf_op jit(solution)/shard_map/bsd,tbshe->tdhe/dot_general | solution.py:68
  1201.3 12.5 all-reduce
  1213.7 70.7 %scatter_custom_fusion = f32[12568,768]{1,0:T(8,128)} fusion(s32[8192]{0:T(1024)S(1)} %bitcast.152, bf16[8192,768]{1,0:T(8,128)(2,1)} %bitcast.149, f32[]{:T(128)} %constant.74.clone.1), kind=kCustom, calls=%fused_computation.7 | custom fusion | flops 12582912 | bytes 51191812 | tf_op jit(solution)/shard_map/scatter-add | solution.py:94
  1284.4 30.1 %all-reduce.3.cloned.1.call-done = f32[2050,768]{1,0:T(8,128)} async-done(((f32[2050,768]{1,0:T(8,128)}), f32[2050,768]{1,0:T(8,128)}) %all-reduce.3.cloned.1.call-update) | async-done | bytes 6297616 | tf_op jit(solution)/shard_map/psum | solution.py:91
  (160 shorter events, 108.5 us)
Async XLA Ops:
  7.2 60.9 %copy-start = (bf16[2050,768]{1,0:T(8,128)(2,1)S(1)}, bf16[2050,768]{1,0:T(8,128)(2,1)}, u32[]{:S(2)}) copy-start(bf16[2050,768]{1,0:T(8,128)(2,1)} %param.20) | copy-start | bytes 9446404
  7.2 152.0 %reduce-scatter.6.cloned.1.call-start = ((), (), s32[]{:S(2)}) async-start(), calls=%async_computation.5 | async-start | bytes 15728640 | tf_op jit(solution)/shard_map/reduce_scatter | solution.py:86
  65.7 182.1 %all-gather.6.cloned.1.call-start = ((), (), s32[]{:S(2)}) async-start(), calls=%async_computation.6 | async-start | bytes 15728640 | tf_op jit(solution)/shard_map/all_gather | solution.py:27
  66.3 98.3 %copy-start.21 = (f32[768]{0:T(1024)}, f32[768]{0:T(1024)S(1)}, u32[]{:S(2)}) copy-start(f32[768]{0:T(1024)S(1)} %convert_element_type.146) | copy-start | bytes 9220
  162.9 266.0 %copy-start.2 = (bf16[32,64,768]{2,1,0:T(8,128)(2,1)}, bf16[32,64,768]{2,1,0:T(8,128)(2,1)S(1)}, u32[]{:S(2)}) copy-start(bf16[32,64,768]{2,1,0:T(8,128)(2,1)S(1)} %get-tuple-element.36) | copy-start | bytes 9437188
  167.7 261.3 %reduce-scatter.8.cloned.1.call-start = ((), (), s32[]{:S(2)}) async-start(), calls=%async_computation.7 | async-start | bytes 15728640 | tf_op jit(solution)/shard_map/reduce_scatter | solution.py:37
  314.8 13.2 copy-start.11
  338.2 178.0 %all-gather.8.cloned.1.call-start = ((), (), s32[]{:S(2)}) async-start(), calls=%async_computation.8 | async-start | bytes 15728640 | tf_op jit(solution)/shard_map/all_gather | solution.py:40
  433.7 82.6 %copy-start.35 = (bf16[768,768]{1,0:T(8,128)(2,1)S(1)}, bf16[768,768]{1,0:T(8,128)(2,1)}, u32[]{:S(2)}) copy-start(bf16[768,768]{1,0:T(8,128)(2,1)} %param.29) | copy-start | bytes 3538948
  436.2 161.5 %all-gather.10.cloned.1.call-start = ((), (), s32[]{:S(2)}) async-start(), calls=%async_computation.10 | async-start | bytes 15728640 | tf_op jit(solution)/shard_map/all_gather | solution.py:46
  436.7 286.7 %reduce-scatter.12.cloned.1.call-start = ((), (), s32[]{:S(2)}) async-start(), calls=%async_computation.11 | async-start | bytes 15728640 | tf_op jit(solution)/shard_map/reduce_scatter | solution.py:54
  436.8 160.8 %copy-start.36 = (bf16[768,768]{1,0:T(8,128)(2,1)S(1)}, bf16[768,768]{1,0:T(8,128)(2,1)}, u32[]{:S(2)}) copy-start(bf16[768,768]{1,0:T(8,128)(2,1)} %param.31) | copy-start | bytes 3538948
  534.2 81.5 %copy-start.40 = (u32[256,768]{1,0:T(8,128)}, u32[256,768]{1,0:T(8,128)S(1)}, u32[]{:S(2)}) copy-start(u32[256,768]{1,0:T(8,128)S(1)} %get-tuple-element.49) | copy-start | bytes 2359300
  632.8 183.9 %reduce-scatter.10.cloned.1.call-start = ((), (), s32[]{:S(2)}) async-start(), calls=%async_computation.9 | async-start | bytes 15728640 | tf_op jit(solution)/shard_map/reduce_scatter | solution.py:43
  650.1 73.4 %copy-start.5 = (bf16[32,64,768]{2,1,0:T(8,128)(2,1)S(1)}, bf16[32,64,768]{2,1,0:T(8,128)(2,1)}, u32[]{:S(2)}) copy-start(bf16[32,64,768]{2,1,0:T(8,128)(2,1)} %copy-done.4) | copy-start | bytes 9437188
  650.1 254.9 %all-gather.12.cloned.1.call-start = ((), (), s32[]{:S(2)}) async-start(), calls=%async_computation.12 | async-start | bytes 15728640 | tf_op jit(solution)/shard_map/all_gather | solution.py:57
  732.7 172.4 %copy-start.38 = (bf16[3,64,768]{2,1,0:T(8,128)(2,1)S(1)}, bf16[3,64,768]{2,1,0:T(8,128)(2,1)}, u32[]{:S(2)}) copy-start(bf16[3,64,768]{2,1,0:T(8,128)(2,1)} %param.25) | copy-start | bytes 884740
  824.9 90.6 %copy-start.12 = (f32[32,3,256]{2,1,0:T(4,128)S(1)}, f32[32,3,256]{2,1,0:T(4,128)}, u32[]{:S(2)}) copy-start(f32[32,3,256]{2,1,0:T(4,128)} %copy-done.11) | copy-start | bytes 294916
  824.9 278.3 %reduce-scatter.14.cloned.1.call-start = ((), (), s32[]{:S(2)}) async-start(), calls=%async_computation.13 | async-start | bytes 15728640 | tf_op jit(solution)/shard_map/reduce_scatter | solution.py:70
  985.1 10.6 copy-start.37
  1012.5 90.7 %copy-start.3 = (bf16[32,64,768]{2,1,0:T(8,128)(2,1)S(1)}, bf16[32,64,768]{2,1,0:T(8,128)(2,1)}, u32[]{:S(2)}) copy-start(bf16[32,64,768]{2,1,0:T(8,128)(2,1)} %copy-done.2) | copy-start | bytes 9437188
  1012.5 90.7 %copy-start.10 = (f32[32,64]{1,0:T(8,128)S(1)}, f32[32,64]{1,0:T(8,128)}, u32[]{:S(2)}) copy-start(f32[32,64]{1,0:T(8,128)} %copy-done.9) | copy-start | bytes 24580
  1012.5 90.7 %copy-start.22 = (f32[768]{0:T(1024)S(1)}, f32[768]{0:T(1024)}, u32[]{:S(2)}) copy-start(f32[768]{0:T(1024)} %copy-done.21) | copy-start | bytes 9220
  1012.5 94.7 %copy-start.17 = (f32[32,64]{1,0:T(8,128)S(1)}, f32[32,64]{1,0:T(8,128)}, u32[]{:S(2)}) copy-start(f32[32,64]{1,0:T(8,128)} %copy-done.16) | copy-start | bytes 24580
  1012.6 94.7 %copy-start.14 = (f32[32,64]{1,0:T(8,128)S(1)}, f32[32,64]{1,0:T(8,128)}, u32[]{:S(2)}) copy-start(f32[32,64]{1,0:T(8,128)} %copy-done.13) | copy-start | bytes 24580
  1012.6 201.2 %all-gather.14.cloned.1.call-start = ((), (), s32[]{:S(2)}) async-start(), calls=%async_computation.14 | async-start | bytes 15728640 | tf_op jit(solution)/shard_map/all_gather | solution.py:92
  1116.6 197.9 %all-reduce.3.cloned.1.call-start = ((), (), s32[]{:S(2)}) async-start(), calls=%async_computation.15 | async-start | bytes 12632064 | tf_op jit(solution)/shard_map/psum | solution.py:91
  1116.8 16.6 %copy-start.41 = (u32[256,768]{1,0:T(8,128)S(1)}, u32[256,768]{1,0:T(8,128)}, u32[]{:S(2)}) copy-start(u32[256,768]{1,0:T(8,128)} %copy-done.40) | copy-start | bytes 2359300
  1185.3 16.0 %copy-start.23 = (f32[768]{0:T(1024)S(1)}, f32[768]{0:T(1024)}, u32[]{:S(2)}) copy-start(f32[768]{0:T(1024)} %get-tuple-element.19) | copy-start | bytes 9220
  1185.3 16.0 %copy-start.24 = (f32[768]{0:T(1024)S(1)}, f32[768]{0:T(1024)}, u32[]{:S(2)}) copy-start(f32[768]{0:T(1024)} %get-tuple-element.15) | copy-start | bytes 9220
  1185.3 16.0 %copy-start.25 = (f32[768]{0:T(1024)S(1)}, f32[768]{0:T(1024)}, u32[]{:S(2)}) copy-start(f32[768]{0:T(1024)} %get-tuple-element.29) | copy-start | bytes 9220
  1185.3 16.0 %copy-start.26 = (f32[768]{0:T(1024)S(1)}, f32[768]{0:T(1024)}, u32[]{:S(2)}) copy-start(f32[768]{0:T(1024)} %get-tuple-element.39) | copy-start | bytes 9220
  (21 other events, 59.9 us)
Sparse Core Ops, SparseCore 0:
  65.8 93.3 reduce-scatter.5
  167.8 79.9 all-gather.5
  338.4 90.5 reduce-scatter.7
  436.3 79.9 all-gather.7
  517.7 79.9 all-gather.9
  632.9 90.5 reduce-scatter.11
  726.0 90.5 reduce-scatter.9
  825.1 79.9 all-gather.11
  1012.7 90.5 reduce-scatter.13
  1116.7 79.9 all-gather.13
  1199.7 114.7 all-reduce.2
where the time goes:
time: 1330 us
  waiting for transfers between devices  750 us (56%)
  matrix products  270 us (20%)
  other arithmetic  214 us (16%)
  local copies, waits for them, and re-layouts  66.3 us (5%)
  between operations  14.5 us (1%)
    reduce_scatter x1, waiting for transfers between devices, layer_pass(): lax.psum_scatter(d_norm1_part, 'tp', scatter_dimension=1, tiled=True)  90.6 us
    reduce_scatter x1, waiting for transfers between devices, layer_pass(): lax.psum_scatter(attn_part, 'tp', scatter_dimension=1, tiled=True)  90 us
    reduce_scatter x1, waiting for transfers between devices, layer_pass(): mlp_rows = lax.psum_scatter(mlp_part, 'tp', scatter_dimension=1, tiled=True)  84 us
    reduce_scatter x1, waiting for transfers between devices, device_step(): emb_rows = lax.psum_scatter(emb_part, 'tp', scatter_dimension=1, tiled=True)  81.7 us
    all_gather x1, waiting for transfers between devices, layer_pass(): d_hidden1_full = lax.all_gather(d_hidden1, 'tp', axis=1, tiled=True)  80.1 us
    all_gather x1, waiting for transfers between devices, layer_pass(): normed2_full = lax.all_gather(normed2, 'tp', axis=1, tiled=True)  79.5 us
    all_gather x1, waiting for transfers between devices, layer_pass(): normed1_full = lax.all_gather(normed1, 'tp', axis=1, tiled=True)  76.9 us
    reduce_scatter x1, waiting for transfers between devices, layer_pass(): lax.psum_scatter(d_norm2_part, 'tp', scatter_dimension=1, tiled=True)  72.7 us
  transfers between devices with their start and end apart: 11, of which 10 were waited for; matrix products, arithmetic and copies ran while one was open for 16% of the time, Pallas kernels for 0%

commit v1 on v0

v1 whole, which is shorter than its diff:
```python
import math
import jax
import jax.numpy as jnp
from jax import lax
from jax.experimental import pallas as pl
from jax.experimental.pallas import tpu as pltpu
from jax.sharding import PartitionSpec as P

LN_EPS = 1e-5
NEG_BIG = -1e30
LANE = 128
VMEM = 62 * 2**20
UNROLL = 4
TP, X, CORE, HALVES, QKV = 4, 2, 1, 2, 3
ROWS = 0
NN, NT, TN = ((1,), (0,)), ((1,), (1,)), ((0,), (0,))
SUB = 8
BATCH = 16
F32 = jnp.float32
BF16 = jnp.bfloat16


def swap(value, step):
    return lax.ppermute(value, 'tp', [(i, i ^ step) for i in range(4)])


def xor_order(value, rank):
    value = jnp.where((rank & 2) > 0, jnp.concatenate([value[2:], value[:2]]), value)
    flipped = jnp.stack([value[1], value[0], value[3], value[2]])
    return jnp.where((rank & 1) > 0, flipped, value)


def dot(a, b, dims, out=F32):
    return lax.dot_general(a, b, (dims, ((), ())), preferred_element_type=F32).astype(out)


def ln_stats(hidden):
    hidden32 = hidden.astype(F32)
    centered = hidden32 - jnp.mean(hidden32, axis=-1, keepdims=True)
    variance = jnp.mean(jnp.square(centered), axis=-1, keepdims=True)
    inv = lax.rsqrt(variance + LN_EPS)
    return centered * inv, inv


def ln_forward(hidden, gain, shift):
    scaled, _ = ln_stats(hidden)
    return (scaled * gain.astype(F32) + shift.astype(F32)).astype(BF16)


def ln_backward(hidden, gain, d_out):
    scaled, inv = ln_stats(hidden)
    d_out = d_out.astype(F32)
    d_gain = jnp.sum(d_out * scaled, axis=0)
    d_shift = jnp.sum(d_out, axis=0)
    d_scaled = d_out * gain.astype(F32)
    mean_d = jnp.mean(d_scaled, axis=-1, keepdims=True)
    mean_ds = jnp.mean(d_scaled * scaled, axis=-1, keepdims=True)
    return (d_scaled - mean_d - scaled * mean_ds) * inv, d_gain, d_shift


def half_of(pair, keep):
    return jnp.where(keep, pair, jnp.zeros_like(pair))


def softmax(scores, allowed, axis):
    scores = jnp.where(allowed, scores, NEG_BIG)
    weights = jnp.exp(scores - jnp.max(scores, axis=axis, keepdims=True))
    return weights * (1.0 / jnp.sum(weights, axis=axis, keepdims=True))


def pair_offsets(width):
    span = width // 6
    return [(half * 3 * span + j, half * 3 * span + span + j, half * 3 * span + 2 * span + j, half * span + j)
            for half in range(2) for j in range(0, span, LANE)]


def allowed_of(mask_ref):
    return mask_ref[0] > 0


def attn_fwd_kernel(mask_ref, qkv_ref, ctx_ref):
    rows, width = mask_ref.shape[1], qkv_ref.shape[-1]
    allowed = allowed_of(mask_ref)
    low = lax.broadcasted_iota(jnp.int32, (rows, LANE), 1) < 64

    def take(start):
        return qkv_ref[:, 0, :, start:start + LANE].reshape(rows, LANE)

    for qo, ko, vo, co in pair_offsets(width):
        q, k, v = take(qo), take(ko), take(vo)
        parts = [dot(softmax(dot(half_of(q, keep), k, NT), allowed, -1).astype(BF16), v, NN) for keep in (low, ~low)]
        ctx = jnp.where(low, parts[0], parts[1]).astype(BF16)
        ctx_ref[:, 0, :, co:co + LANE] = ctx.reshape(ctx_ref.shape[0], -1, LANE)


def attn_bwd_kernel(q_scale, mask_ref, qkv_ref, dctx_ref, dqkv_ref, bias_ref):
    rows, width = mask_ref.shape[1], qkv_ref.shape[-1]
    allowed = allowed_of(mask_ref)
    low = lax.broadcasted_iota(jnp.int32, (rows, LANE), 1) < 64

    @pl.when(pl.program_id(0) == 0)
    def _():
        bias_ref[...] = jnp.zeros_like(bias_ref)

    def take(ref, start):
        return ref[:, 0, :, start:start + LANE].reshape(rows, LANE)

    def put(start, value):
        bias_ref[0:1, start:start + LANE] += jnp.sum(value, axis=ROWS, keepdims=True)
        dqkv_ref[:, 0, :, start:start + LANE] = value.astype(BF16).reshape(dqkv_ref.shape[0], -1, LANE)

    for qo, ko, vo, co in pair_offsets(width):
        q, k, v = take(qkv_ref, qo), take(qkv_ref, ko), take(qkv_ref, vo)
        dc = take(dctx_ref, co)
        parts = []
        for keep in (low, ~low):
            probs = softmax(dot(k, half_of(q, keep), NT), allowed, 0)
            d_probs = dot(v, half_of(dc, keep), NT)
            d_scores = (probs * (d_probs - jnp.sum(d_probs * probs, axis=ROWS, keepdims=True))).astype(BF16)
            parts.append((dot(d_scores, k, TN) * q_scale, dot(d_scores, q, NN), dot(probs.astype(BF16), dc, NN)))
        for start, a, b in zip((qo, ko, vo), *parts):
            put(start, jnp.where(low, a, b))


def seq_spec(width, seq_local, chunk=None):
    if chunk is None:
        return pl.BlockSpec((4, 1, seq_local, width), lambda s: (0, s, 0, 0))
    return pl.BlockSpec((None, 4, 1, seq_local, width), lambda s: (chunk, 0, s, 0, 0))


def mask_spec(seq, chunk, n_seq):
    return pl.BlockSpec((1, seq, seq), lambda s: (chunk * n_seq + s, 0, 0))


def attn_forward(allowed, qkv, chunk):
    _, n_seq, seq_local, width = qkv.shape
    seq = 4 * seq_local
    return pl.pallas_call(
        attn_fwd_kernel, grid=(n_seq,),
        out_shape=jax.ShapeDtypeStruct((4, n_seq, seq_local, width // 3), BF16),
        in_specs=[mask_spec(seq, chunk, n_seq), seq_spec(width, seq_local)],
        out_specs=seq_spec(width // 3, seq_local),
        cost_estimate=pl.CostEstimate(flops=n_seq * 12 * seq * seq * 512, bytes_accessed=qkv.size * 3, transcendentals=ROWS),
        name='attn_fwd')(allowed, qkv)


def attn_backward(allowed, qkv, d_ctx, chunk, q_scale):
    _, n_seq, seq_local, width = qkv.shape
    seq = 4 * seq_local
    return pl.pallas_call(
        lambda *refs: attn_bwd_kernel(q_scale, *refs), grid=(n_seq,),
        out_shape=[jax.ShapeDtypeStruct(qkv.shape, BF16), jax.ShapeDtypeStruct((8, width), F32)],
        in_specs=[mask_spec(seq, chunk, n_seq), seq_spec(width, seq_local), seq_spec(width // 3, seq_local, chunk)],
        out_specs=[seq_spec(width, seq_local), pl.BlockSpec((8, width), lambda s: (0, 0))],
        cost_estimate=pl.CostEstimate(flops=n_seq * 12 * seq * seq * 1280, bytes_accessed=qkv.size * 6, transcendentals=ROWS),
        name='attn_bwd')(allowed, qkv, d_ctx)


def group_rows(lanes):
    return -(-(lanes * (SUB + 1)) // SUB) * SUB


def row_slice(start, lanes):
    return pl.ds(start, lanes, stride=SUB + 1)


def tile_loop(rows, lanes, body):
    def step(t, _):
        for j in range(lanes):
            body(pl.ds(pl.multiple_of(t * 2 * SUB, 2 * SUB), 2 * SUB), [(2 * t + h) * group_rows(lanes) + j * (SUB + 1) for h in range(2)], pl.ds(j * LANE, LANE))
        return 0

    lax.fori_loop(0, rows // (2 * SUB), step, 0, unroll=2)


def spread(dst_ref, start, src_ref):
    def body(rows, groups, cols):
        piece = src_ref[rows, cols].astype(F32)
        for h, at in enumerate(groups):
            dst_ref[pl.ds(start + at, SUB), :] = piece[h * SUB:(h + 1) * SUB]

    tile_loop(src_ref.shape[0], src_ref.shape[1] // LANE, body)


def collect(dst_ref, src_ref):
    def body(rows, groups, cols):
        dst_ref[rows, cols] = jnp.concatenate([src_ref[pl.ds(at, SUB), :] for at in groups]).astype(dst_ref.dtype)

    tile_loop(dst_ref.shape[0], dst_ref.shape[1] // LANE, body)


def placed(ids, lanes):
    return (ids // SUB) * group_rows(lanes) + ids % SUB


def gather_kernel(first, block, at_ref, table_ref, *refs):
    outs, (held_ref, rows_ref) = refs[:-2], refs[-2:]
    lanes = table_ref.shape[1] // LANE
    group = group_rows(lanes)
    step = pl.program_id(0)
    per = (pl.num_programs(0) - first) // len(outs)

    @pl.when(step < first)
    def _():
        held_ref[held_ref.shape[0] - group:, :] = jnp.zeros((group, LANE), F32)
        spread(held_ref, step * (table_ref.shape[0] // SUB * group), table_ref)

    @pl.when(step >= first)
    def _():
        def take(batch, _):
            for i in range(BATCH):
                row = held_ref[row_slice(at_ref[(step - first) * block + batch * BATCH + i], lanes), :]
                rows_ref[row_slice((batch * (BATCH // SUB) + i // SUB) * group + i % SUB, lanes), :] = row
            return 0

        lax.fori_loop(0, block // BATCH, take, 0)
        for k, out in enumerate(outs):
            pl.when((step - first) // per == k)(lambda out=out: collect(out, rows_ref))


def gather(table, ids, owned, n_out, block=512, table_block=1024):
    vocab_local, d = table.shape
    first, lanes, per = -(-vocab_local // table_block), d // LANE, ids.size // (n_out * block)
    at = placed(jnp.where(owned, ids, first * table_block), lanes)
    group = group_rows(lanes)

    def out_spec(k):
        return pl.BlockSpec((block, d), lambda s, *_: (jnp.clip(s - first - k * per, 0, per - 1), 0))

    return pl.pallas_call(
        lambda *refs: gather_kernel(first, block, *refs),
        grid_spec=pltpu.PrefetchScalarGridSpec(
            num_scalar_prefetch=1, grid=(first + n_out * per,),
            in_specs=[pl.BlockSpec((table_block, d), lambda s, *_: (jnp.minimum(s, first - 1), 0))],
            out_specs=[out_spec(k) for k in range(n_out)],
            scratch_shapes=[pltpu.VMEM(((first * table_block // SUB + 1) * group, LANE), F32), pltpu.VMEM((block // SUB * group, LANE), F32)]),
        out_shape=[jax.ShapeDtypeStruct((per * block, d), BF16)] * n_out,
        compiler_params=pltpu.CompilerParams(vmem_limit_bytes=VMEM),
        name='emb_gather')(at.reshape(-1), table)


def scatter_kernel(n_src, n_tiles, block, out_tiles, ids_ref, repeat_ref, *refs):
    srcs, (out_ref, acc_ref, rows_ref, stage_ref, sem) = refs[:n_src], refs[n_src:]
    step = pl.program_id(0)
    lanes = stage_ref.shape[-1] // LANE
    group = group_rows(lanes)
    per_src = pl.num_programs(0) // n_src

    @pl.when(step == 0)
    def _():
        def clear(i, _):
            acc_ref[pl.ds(pl.multiple_of(i * group, SUB), group), :] = jnp.zeros((group, LANE), F32)
            return 0

        lax.fori_loop(0, acc_ref.shape[0] // group, clear, 0, unroll=UNROLL)

    for k, src in enumerate(srcs):
        pl.when(step // per_src == k)(lambda src=src: spread(rows_ref, 0, src))

    def add(batch, _):
        first = step * block + batch * BATCH
        tiles = BATCH // SUB
        slots = [acc_ref.at[row_slice(ids_ref[first + i], lanes), :] for i in range(BATCH)]
        rows = [rows_ref.at[row_slice((batch * tiles + i // SUB) * group + i % SUB, lanes), :] for i in range(BATCH)]
        repeats = repeat_ref[step * (block // BATCH) + batch]

        @pl.when(repeats == 0)
        def _():
            sums = [slot[...] + row[...] for slot, row in zip(slots, rows)]
            for slot, total in zip(slots, sums):
                slot[...] = total

        @pl.when(repeats != 0)
        def _():
            for slot, row in zip(slots, rows):
                slot[...] += row[...]

        return 0

    lax.fori_loop(0, block // BATCH, add, 0)

    @pl.when(step == pl.num_programs(0) - 1)
    def _():
        n_out, rest = divmod(n_tiles, out_tiles)

        def copy(start, slot, size):
            return pltpu.make_async_copy(stage_ref.at[slot, pl.ds(0, size)], out_ref.at[pl.ds(start, size)], sem.at[slot])

        def stage(start, slot, size):
            def move(t, _):
                for j in range(lanes):
                    stage_ref[slot, t, :, pl.ds(j * LANE, LANE)] = acc_ref[pl.ds((start + t) * group + j * (SUB + 1), SUB), :]
                return 0

            lax.fori_loop(0, size, move, 0, unroll=UNROLL if size % UNROLL == 0 else 1)

        def flush(i, _):
            slot = lax.rem(i, 2)

            @pl.when(i >= 2)
            def _():
                copy((i - 2) * out_tiles, slot, out_tiles).wait()

            stage(i * out_tiles, slot, out_tiles)
            copy(i * out_tiles, slot, out_tiles).start()
            return 0

        lax.fori_loop(0, n_out, flush, 0)
        copy((n_out - 2) * out_tiles, n_out % 2, out_tiles).wait()
        if rest:
            stage(n_out * out_tiles, n_out % 2, rest)
            copy(n_out * out_tiles, n_out % 2, rest).start()
        copy((n_out - 1) * out_tiles, (n_out - 1) % 2, out_tiles).wait()
        if rest:
            copy(n_out * out_tiles, n_out % 2, rest).wait()


def repeats(ids, vocab_local):
    batch = ids.reshape(-1, BATCH)
    same = jnp.zeros(batch.shape[:1], bool)
    for i in range(1, BATCH):
        same |= jnp.any((batch[:, i:] == batch[:, :-i]) & (batch[:, i:] < vocab_local), axis=1)
    return same.astype(jnp.int32)


def scatter(ids, repeat, srcs, vocab_local, block=512):
    rows, d = srcs[0].shape
    n_src = len(srcs)
    n_tiles = vocab_local // SUB
    out_tiles = 64
    per = rows // block
    lanes = d // 128
    group = group_rows(lanes)

    def spec(k):
        return pl.BlockSpec((block, d), lambda s, *_: (jnp.clip(s - k * per, 0, per - 1), 0))

    out = pl.pallas_call(
        lambda *r: scatter_kernel(n_src, n_tiles, block, out_tiles, *r),
        grid_spec=pltpu.PrefetchScalarGridSpec(num_scalar_prefetch=2, grid=(n_src * per,),
            in_specs=[spec(k) for k in range(n_src)], out_specs=pl.BlockSpec(memory_space=pl.ANY),
            scratch_shapes=[pltpu.VMEM(((n_tiles + 1) * group, 128), F32), pltpu.VMEM((block // SUB * group, 128), F32),
                            pltpu.VMEM((2, out_tiles, SUB, d), F32), pltpu.SemaphoreType.DMA((2,))]),
        out_shape=jax.ShapeDtypeStruct((n_tiles, SUB, d), F32),
        compiler_params=pltpu.CompilerParams(vmem_limit_bytes=VMEM),
        cost_estimate=pl.CostEstimate(flops=50 * 10**9, bytes_accessed=4 * vocab_local * d, transcendentals=ROWS),
        name='emb_scatter')(placed(ids, lanes), repeat, *srcs)
    return out.reshape(vocab_local, d)


def ff_slices(width, block=512):
    return [pl.ds(i * block, block) for i in range(width // block)]


def zero_first(*refs):
    @pl.when(pl.program_id(0) == 0)
    def _():
        for ref in refs:
            ref[...] = jnp.zeros_like(ref)


def at_last(ref, total_ref):
    @pl.when(pl.program_id(0) == pl.num_programs(0) - 1)
    def _():
        ref[...] = total_ref[...].astype(ref.dtype)


def add_row(ref, index, value, cols=slice(None)):
    ref[pl.ds(index, 1), cols] += jnp.sum(value, axis=ROWS, keepdims=True)


def chunk_tile(refs):
    tile = refs[0][...]
    for c, ref in enumerate(refs):
        tile = jnp.where(pl.program_id(0) * len(refs) >= c * pl.num_programs(0), ref[...], tile)
    return tile


def mlp_forward_kernel(*refs):
    h0_refs, ctx_refs, refs = refs[:2], refs[2:4], refs[4:]
    g_ref, wout_ref, w1n_ref, w1f_ref, w2n_ref, w2f_ref, vec_ref, b1_ref = refs[:8]
    out_ref, h1_ref, n2_ref, dpren_ref, dpref_ref, dw2n_ref, dw2f_ref, db1_ref, sum_ref, far_ref = refs[8:]
    zero_first(dw2n_ref, far_ref, db1_ref, sum_ref)
    b_out, gain, shift, b_fc2 = (vec_ref[i:i + 1] for i in range(4))
    grad = g_ref[...]
    hidden1 = (chunk_tile(h0_refs).astype(F32) + dot(chunk_tile(ctx_refs), wout_ref[...], NN) + b_out).astype(BF16)
    h1_ref[...] = hidden1
    scaled, _ = ln_stats(hidden1)
    normed2 = (scaled * gain + shift).astype(BF16)
    n2_ref[...] = normed2
    total = hidden1.astype(F32) + b_fc2
    halves = ((w1n_ref, w2n_ref, dpren_ref, dw2n_ref), (w1f_ref, w2f_ref, dpref_ref, far_ref))
    for half, (w1_ref, w2_ref, dpre_ref, dw2_ref) in enumerate(halves):
        for cols in ff_slices(w1_ref.shape[0]):
            inner = dot(normed2, w1_ref[cols, :], NT) + b1_ref[half:half + 1, cols]
            inner = jnp.maximum(inner, 0.0).astype(BF16)
            total += dot(inner, w2_ref[cols, :], NN)
            dw2_ref[cols, :] += dot(inner, grad, TN)
            d_pre = jnp.where(inner > 0, dot(grad, w2_ref[cols, :], NT), 0.0)
            add_row(db1_ref, half, d_pre, cols)
            dpre_ref[:, cols] = d_pre.astype(BF16)
    out_ref[...] = total.astype(BF16)
    add_row(sum_ref, 0, grad.astype(F32))
    at_last(dw2f_ref, far_ref)


def mlp_backward_kernel(*refs):
    ctx_refs, refs = refs[:2], refs[2:]
    dpren_ref, dpref_ref, n2_ref, h1_ref, g_ref, w1n_ref, w1f_ref, wout_ref, gain_ref = refs[:9]
    dh1_ref, dctx_ref, dw1n_ref, dw1f_ref, dwon_ref, dwof_ref, sum_ref, w1far_ref, wofar_ref = refs[9:]
    zero_first(dw1n_ref, dwon_ref, w1far_ref, wofar_ref, sum_ref)
    normed2 = n2_ref[...]
    d_norm2 = jnp.zeros(normed2.shape, F32)
    for w1_ref, dpre_ref, dw1_ref in ((w1n_ref, dpren_ref, dw1n_ref), (w1f_ref, dpref_ref, w1far_ref)):
        for cols in ff_slices(w1_ref.shape[0]):
            d_pre = dpre_ref[:, cols]
            d_norm2 += dot(d_pre, w1_ref[cols, :], NN)
            dw1_ref[cols, :] += dot(d_pre, normed2, TN)
    d_norm2 = d_norm2.astype(BF16).astype(F32)
    scaled, inv = ln_stats(h1_ref[...])
    add_row(sum_ref, 0, d_norm2 * scaled)
    add_row(sum_ref, 1, d_norm2)
    d_scaled = d_norm2 * gain_ref[...]
    mean_d = jnp.mean(d_scaled, axis=-1, keepdims=True)
    mean_ds = jnp.mean(d_scaled * scaled, axis=-1, keepdims=True)
    d_hidden1 = (g_ref[...].astype(F32) + (d_scaled - mean_d - scaled * mean_ds) * inv).astype(BF16)
    dh1_ref[...] = d_hidden1
    add_row(sum_ref, 2, d_hidden1.astype(F32))
    context = chunk_tile(ctx_refs)
    half = dwon_ref.shape[0]
    dwon_ref[...] += dot(context[:, :half], d_hidden1, TN)
    wofar_ref[...] += dot(context[:, half:], d_hidden1, TN)
    dctx_ref[...] = dot(d_hidden1, wout_ref[...], NT).astype(BF16)
    at_last(dw1f_ref, w1far_ref)
    at_last(dwof_ref, wofar_ref)


TILE = 512


def row_spec(array):
    return pl.BlockSpec((TILE, array.shape[1]), lambda s: (s, 0))


def chunk_specs(arrays):
    per = arrays[0].shape[0] // TILE
    return [pl.BlockSpec((TILE, a.shape[1]), lambda s, c=c: (jnp.clip(s - c * per, 0, per - 1), 0)) for c, a in enumerate(arrays)]


def whole_spec(array):
    return pl.BlockSpec(array.shape, lambda s: (0,) * len(array.shape), pipeline_mode=pl.Buffered(1))


def fused_call(kernel, chunked, tiled, whole, tiled_out, whole_out, scratch, flops):
    rows = tiled[0].shape[0]
    return pl.pallas_call(
        kernel, grid=(rows // TILE,),
        in_specs=sum([chunk_specs(a) for a in chunked], []) + [row_spec(a) for a in tiled] + [whole_spec(a) for a in whole],
        out_shape=tiled_out + whole_out,
        out_specs=[row_spec(a) for a in tiled_out] + [whole_spec(a) for a in whole_out],
        scratch_shapes=[pltpu.VMEM(a, F32) for a in scratch],
        compiler_params=pltpu.CompilerParams(vmem_limit_bytes=VMEM),
        cost_estimate=pl.CostEstimate(flops=flops, bytes_accessed=10**8, transcendentals=ROWS),
    )(*sum(chunked, []), *tiled, *whole)


def mlp_forward(hidden0, context, grad, wout, w1, w2, vectors, b1):
    rows, d = grad.shape
    ff = w1[0].shape[0]
    like = jax.ShapeDtypeStruct
    tiled_out = [like((rows, d), BF16)] * 3 + [like((rows, ff), BF16)] * 2
    whole_out = [like((ff, d), F32), like((ff, d), BF16), like((SUB, ff), F32), like((SUB, d), F32)]
    return fused_call(mlp_forward_kernel, [hidden0, context], [grad], [wout, *w1, *w2, vectors, b1],
                      tiled_out, whole_out, [(ff, d)], 2 * rows * d * (d + 8 * ff))


def mlp_backward(context, d_pre, normed2, hidden1, grad, w1, wout, gain):
    rows, d = grad.shape
    ff = w1[0].shape[0]
    like = jax.ShapeDtypeStruct
    whole_out = [like((ff, d), F32), like((ff, d), BF16), like((d // 2, d), F32), like((d // 2, d), BF16), like((SUB, d), F32)]
    return fused_call(mlp_backward_kernel, [context], [*d_pre, normed2, hidden1, grad], [*w1, wout, gain],
                      [like((rows, d), BF16)] * 2, whole_out, [(ff, d), (d // 2, d)], 2 * rows * d * (2 * d + 4 * ff))


def fetch(own, y_rank):
    half = own.shape[0] // 2
    mine = swap(lax.dynamic_slice_in_dim(own, y_rank * half, half), 2)
    other = lax.ppermute(mine, 'dp', [(0, 1), (1, 0)])
    first = y_rank == 0
    far = jnp.concatenate([jnp.where(first, mine, other), jnp.where(first, other, mine)])
    near = jnp.stack([own, far])
    return near, swap(near, 1)


def solution(mesh):
    def device_body(tokens, attn_mask, emb_local, pos_table, ln1_gain, ln1_shift, w_qkv, b_qkv, w_out, b_out, ln2_gain, ln2_shift, w_fc1, b_fc1, w_fc2, b_fc2, grad_y):
        vocab_local, d_model = emb_local.shape
        n_all, seq = tokens.shape
        n_seq, seq_local = n_all // TP, seq // TP
        local_heads, e = w_qkv.shape[2:]
        n_heads = 4 * local_heads
        rows = n_seq * seq
        n_chunk = 2
        c_seq, c_rows = n_seq // n_chunk, rows // n_chunk
        hidden = local_heads * e
        ff_local = w_fc2.shape[0]
        q_scale = 1.0 / math.sqrt(e)
        rank = lax.axis_index('tp')
        y_rank = lax.axis_index('dp')
        barrier = lax.optimization_barrier

        qkv_rows = w_qkv.transpose(0, 2, 3, 1).reshape(-1, d_model)
        n_qkv = qkv_rows.shape[0]
        bias_rows = jnp.concatenate([b_qkv.reshape(-1), b_fc1])
        bias_rows = jnp.pad(bias_rows, (0, 32 * d_model - bias_rows.shape[0])).reshape(32, d_model)
        near, far = fetch(jnp.concatenate([qkv_rows, w_out.reshape(-1, d_model), bias_rows]), y_rank)
        pack1 = jnp.stack([near, far])
        wqkv = pack1[:, :, :n_qkv].reshape(HALVES, HALVES, QKV, hidden, d_model).transpose(0, 2, 1, 3, 4).reshape(-1, d_model)
        wout = pack1[:, :, n_qkv:n_qkv + hidden].reshape(-1, d_model)
        biases = pack1[:, :, n_qkv + hidden:].reshape(HALVES, HALVES, -1)
        bqkv = biases[:, :, :n_qkv].reshape(HALVES, HALVES, QKV, hidden).transpose(0, 2, 1, 3).reshape(-1).astype(F32)
        bfc1 = biases[:, :, n_qkv:n_qkv + ff_local].reshape(2, -1).astype(F32)

        canon = tokens.reshape(TP, n_chunk, c_seq, TP, seq_local)
        ids = jnp.stack([jnp.stack([canon[d, :, :, d ^ k] for k in range(TP)], axis=1) for d in range(TP)])
        ids = xor_order(ids, rank).reshape(TP, rows)
        local_ids = ids - rank * vocab_local
        owned = (local_ids >= 0) & (local_ids < vocab_local)

        def chunk(array, c):
            return lax.slice_in_dim(array, c * c_rows, (c + 1) * c_rows)

        diag_part, x_part, core_part, own_part = gather(emb_local, local_ids[::-1], owned[::-1], TP)
        to_x = swap(diag_part, CORE)
        from_x = [swap(chunk(x_part, c) + chunk(to_x, c), X) for c in range(n_chunk)]
        from_near = own_part + swap(core_part, CORE)
        w1_rows, w2_rows, grad_in = w_fc1.T, w_fc2, grad_y
        w1_near, w1_far = (a.reshape(-1, d_model) for a in fetch(w1_rows, y_rank))
        w2_near, w2_far = (a.reshape(-1, d_model) for a in fetch(w2_rows, y_rank))
        grad_in = grad_in.reshape(TP, n_seq, seq_local, d_model)
        g = [lax.dynamic_index_in_dim(grad_in, rank ^ k, 0, keepdims=False) for k in range(TP)]
        g = [g[0]] + [swap(g[k], k) for k in (1, 2, 3)]
        grad = jnp.stack([a.reshape(n_chunk, c_seq, seq_local, d_model) for a in g], axis=1).reshape(rows, d_model)

        mask_all = attn_mask.reshape(TP, n_seq, seq)
        mask = lax.dynamic_index_in_dim(mask_all, rank, 0, keepdims=False)
        positions = jnp.cumsum(mask, axis=1) * mask + 1
        block_of = jnp.arange(TP) ^ rank
        pos_index = (block_of[:, None] * seq_local + jnp.arange(seq_local)[None]).reshape(seq)
        key_mask = xor_order(mask.reshape(n_seq, TP, seq_local).transpose(1, 0, 2), rank).transpose(1, 0, 2).reshape(n_seq, seq)
        causal = pos_index[:, None] >= pos_index[None, :]
        diagonal = jnp.eye(seq, dtype=bool)
        allowed = (causal & ((key_mask[:, None, :] > 0) | diagonal)).astype(F32)
        allowed_t = (causal.T & ((key_mask[:, :, None] > 0) | diagonal)).astype(F32)

        n_pos = -(-(seq + 2) // 8) * 8
        pos_rel = xor_order(positions.reshape(n_chunk, c_seq, TP, seq_local).transpose(2, 0, 1, 3), rank).transpose(1, 0, 2, 3).reshape(rows)
        one_hot = (pos_rel[:, None] == jnp.arange(n_pos)[None]).astype(BF16)
        pos_rows = dot(one_hot, pos_table[:n_pos], NN)

        is_query = (jnp.arange(3 * n_heads * e) // (2 * hidden)) % 3 == 0
        near_rows = from_near.astype(F32) + pos_rows
        hidden0, normed1, qkv, context = [], [], [], []
        for c in range(n_chunk):
            hidden0.append((chunk(near_rows, c) + from_x[c].astype(F32)).astype(BF16))
            normed1.append(ln_forward(hidden0[c], ln1_gain, ln1_shift))
            projected = dot(normed1[c], wqkv, NT) + bqkv
            qkv.append((projected * jnp.where(is_query, q_scale, 1.0)).astype(BF16).reshape(TP, c_seq, seq_local, -1))
            context.append(attn_forward(allowed, qkv[c], c).reshape(c_rows, -1))
            if c + 1 < n_chunk:
                context[c], from_x[c + 1] = barrier((context[c], from_x[c + 1]))
        w1, w2 = (w1_near, w1_far), (w2_near, w2_far)
        vectors = jnp.stack([b_out, ln2_gain, ln2_shift, b_fc2]).astype(F32)
        out, hidden1, normed2, dpre_near, dpre_far, near, far, d_b_fc1, sum_grad = mlp_forward(hidden0, context, grad, wout, w1, w2, vectors, bfc1)
        near_w2, far_w2 = near, far
        out = out.reshape(n_chunk, TP, c_seq, seq_local, d_model)
        out_rows = jnp.zeros((TP, n_seq, seq_local, d_model), BF16)
        for k in range(TP):
            got = out[:, k].reshape(n_seq, seq_local, d_model)
            got = got if k == 0 else swap(got, k)
            out_rows = lax.dynamic_update_index_in_dim(out_rows, got, rank ^ k, 0)
        out_rows = out_rows.reshape(n_all, seq_local, d_model)

        def start_reduce(near, far, lead=1):
            near = (near + swap(far, CORE).astype(F32)).reshape(lead, HALVES, -1, d_model)
            return near[:, 0], near[:, 1].astype(BF16)

        def end_reduce(own, to_send):
            return (own + swap(to_send, 2).astype(F32)).reshape(-1, d_model)

        g_w2 = start_reduce(near_w2, far_w2)
        d_hidden1, d_context, near, far, near_out, far_out, sums = mlp_backward(context, (dpre_near, dpre_far), normed2, hidden1, grad, w1, wout, vectors[1:2])
        g_w1, g_wout = start_reduce(near, far), start_reduce(near_out, far_out)
        d_context = d_context.reshape(n_chunk, TP, c_seq, seq_local, -1)
        d_b_qkv, d_hidden0, d_ln1_gain, d_ln1_shift, near, far = 0.0, [], 0.0, 0.0, 0.0, 0.0
        for c in range(n_chunk):
            d_qkv, d_bias = attn_backward(allowed_t, qkv[c], d_context, c, q_scale)
            d_b_qkv = d_b_qkv + d_bias[ROWS]
            d_qkv = d_qkv.reshape(c_rows, -1)
            d_norm1 = dot(d_qkv, wqkv, NN, BF16)
            d_hidden0_ln, d_gain, d_shift = ln_backward(hidden0[c], ln1_gain, d_norm1)
            d_ln1_gain, d_ln1_shift = d_ln1_gain + d_gain, d_ln1_shift + d_shift
            d_hidden0.append((chunk(d_hidden1, c).astype(F32) + d_hidden0_ln).astype(BF16))
            if c + 1 < n_chunk:
                d_hidden0[c], d_context = barrier((d_hidden0[c], d_context))
            width = 6 * hidden
            near = near + dot(d_qkv[:, :width], normed1[c], TN)
            far = far + dot(d_qkv[:, width:], normed1[c], TN)
        g_wqkv = start_reduce(near, far.astype(BF16), 3)

        d_pos = sum(dot(chunk(one_hot, c), d_hidden0[c], TN) for c in range(n_chunk))
        vectors = jnp.stack([d_ln1_gain, d_ln1_shift, sums[2], sums[0], sums[1], sum_grad[0]])
        hid_b = d_b_qkv.reshape(HALVES, QKV, HALVES, hidden).transpose(0, 2, 1, 3).reshape(TP, -1)
        block_b = jnp.concatenate([hid_b, d_b_fc1[:2].reshape(TP, -1)], axis=1)
        block_b = jnp.stack([block_b[0], block_b[2], block_b[1], block_b[3]])
        block_b = xor_order(block_b, rank)
        small = jnp.concatenate([vectors.reshape(-1), block_b.reshape(-1)])
        small = jnp.pad(small, (0, -small.shape[0] % (16 * d_model))).reshape(-1, d_model)
        total = jnp.concatenate([d_pos, small])
        total = total + swap(total, CORE)

        own_ids = jnp.where(owned, local_ids, vocab_local)
        x_rows = [swap(d_hidden0[c], X) for c in range(n_chunk)]
        total = total + swap(total, X)
        all_rows = d_hidden0 + [swap(a, CORE) for a in d_hidden0] + x_rows + [swap(a, CORE) for a in x_rows]
        d_emb = scatter(own_ids.reshape(-1), repeats(own_ids, vocab_local), all_rows, vocab_local)
        d_pos = jnp.pad(total[:n_pos], ((0, pos_table.shape[0] - n_pos), (0, 0)))
        vectors = total[n_pos:n_pos + 6]
        blocks = total[n_pos + 6:].reshape(-1)[:block_b.size].reshape(block_b.shape)
        own_b = lax.dynamic_index_in_dim(blocks, rank, 0, keepdims=False)
        d_w_qkv = end_reduce(*g_wqkv).reshape(3, local_heads, e, d_model).transpose(0, 3, 1, 2)
        d_w_out, d_w_fc1, d_w_fc2 = (end_reduce(*a) for a in (g_wout, g_w1, g_w2))
        return (out_rows, d_emb, d_pos, vectors[0], vectors[1], d_w_qkv, own_b[:3 * hidden].reshape(3, local_heads, e), d_w_out.reshape(local_heads, e, d_model), vectors[2], vectors[3], vectors[4], d_w_fc1.T, own_b[3 * hidden:], d_w_fc2, vectors[5])

    vec, part, heads = P(None), P('tp', None), P(None, 'tp', None)
    in_specs = (P('dp', None), P('dp', None), part, P(None, None), vec, vec, P(None, None, 'tp', None), heads, P('tp', None, None), vec, vec, vec, P(None, 'tp'), P('tp'), part, vec, P('dp', 'tp', None))
    sums, split = P('dp'), P(('dp', 'tp'), None)
    out_specs = (P('dp', 'tp', None), split, P('dp', None), sums, sums, P('dp', None, 'tp', None), P('dp', 'tp', None), P(('dp', 'tp'), None, None), sums, sums, sums, P('dp', 'tp'), P(('dp', 'tp')), split, sums)
    return jax.shard_map(device_body, mesh=mesh, in_specs=in_specs, out_specs=out_specs, check_vma=False)
```

time: 1330 us -> 649 us (0.49)
  waiting for transfers between devices: 750 us -> 211 us
  Pallas kernels: 0 us -> 250 us
  matrix products: 270 us -> 54.3 us
  other arithmetic: 214 us -> 64.7 us
  local copies, waits for them, and re-layouts: 66.3 us -> 32.5 us
  starting transfers between devices: 0.74 us -> 25.2 us
    reduce_scatter x5 -> x0, waiting for transfers between devices: 419 us -> none  [the longest x1 90.6 us: layer_pass(): lax.psum_scatter(d_norm1_part, 'tp', scatter_dimension=1, tiled=True)]
    all_gather x5 -> x0, waiting for transfers between devices: 300 us -> none  [the longest x1 80.1 us: layer_pass(): d_hidden1_full = lax.all_gather(d_hidden1, 'tp', axis=1, tiled=True)]
    pallas_call x0 -> x8, Pallas kernels: none -> 250 us  [the longest x2 97.9 us: fused_call(): pl.pallas_call(kernel, grid=(rows // TILE,), in_specs=sum([chunk_specs(a)...]
    dot_general x18 -> x11, matrix products: 270 us -> 54.3 us  [dot(): lax.dot_general(a, b, (dims, ((), ())), preferred_element_type=F32)]
    ppermute x0 -> x35, waiting for transfers between devices: none -> 211 us  [the longest x32 203 us: swap(): return lax.ppermute(value, 'tp', [(i, i ^ step) for i in range(4)])]
    scatter-add x2 -> x0, other arithmetic: 89.3 us -> none  [the longest x1 70.7 us: device_step(): jax.ops.segment_sum(d_hidden0_full.astype(jnp.float32).reshape(-1, d_mode...]
    gather x2 -> x0, local copies, waits for them, and re-layouts: 55.4 us -> none  [the longest x1 46 us: device_step(): jnp.take(emb_local, jnp.where(is_owned, local_ids, 0), axis=0)]
    reduce_sum x10 -> x4, other arithmetic: 42.4 us -> 6.93 us  [the longest x2 5.73 us: ln_stats(): centered = hidden32 - jnp.mean(hidden32, axis=-1, keepdims=True)]
  transfers between devices with their start and end apart: 11 -> 35, of which waited for: 10 -> 13; matrix products, arithmetic and copies ran while one was open for 16% -> 21% of each run, Pallas kernels for 0% -> 15%
where the time goes in v1:
time: 649 us; the launch traced here: 640 us
  Pallas kernels  250 us (39%)
  waiting for transfers between devices  211 us (33%)
  other arithmetic  64.7 us (10%)
  matrix products  54.3 us (8%)
  local copies, waits for them, and re-layouts  32.5 us (5%)
  starting transfers between devices  25.2 us (4%)
    ppermute x32, waiting for transfers between devices, swap(): return lax.ppermute(value, 'tp', [(i, i ^ step) for i in range(4)])  203 us
    pallas_call x2, Pallas kernels, fused_call(): pl.pallas_call(kernel, grid=(rows // TILE,), in_specs=sum([chunk_specs(a)...  97.9 us
    pallas_call x1, Pallas kernels, scatter(): pl.pallas_call(lambda *r: scatter_kernel(n_src, n_tiles, block, out_tiles...  54.6 us
    dot_general x11, matrix products, dot(): lax.dot_general(a, b, (dims, ((), ())), preferred_element_type=F32)  54.3 us
    pallas_call x2, Pallas kernels, attn_backward(): pl.pallas_call(lambda *refs: attn_bwd_kernel(q_scale, *refs), grid=(n_seq...  45.5 us
    pallas_call x1, Pallas kernels, gather(): pl.pallas_call(lambda *refs: gather_kernel(first, block, *refs), grid_spe...  31.5 us
    pallas_call x2, Pallas kernels, attn_forward(): pl.pallas_call(attn_fwd_kernel, grid=(n_seq,), out_shape=jax.ShapeDtypeSt...  20.8 us
    ppermute x32, starting transfers between devices, swap(): return lax.ppermute(value, 'tp', [(i, i ^ step) for i in range(4)])  20.1 us
  transfers between devices with their start and end apart: 35, of which 13 were waited for; matrix products, arithmetic and copies ran while one was open for 21% of the time, Pallas kernels for 15%

profile of v1, /device:TPU:0, one launch (start us, length us, event | category | flops | bytes accessed | tf_op | source)
XLA Modules:
  0.0 639.6 jit_solution(2170631127622528369)
XLA Ops:
  4.1 31.5 %emb_gather.1 = (bf16[2048,768]{1,0:T(8,128)(2,1)}, bf16[2048,768]{1,0:T(8,128)(2,1)}, bf16[2048,768]{1,0:T(8,128)(2,1)}, bf16[2048,768]{1,0:T(8,128)(2,1)}) custom-call(s32[8192]{0:T(1024)} %bitcast.243, bf16[12568,768]{1,0:T(8,128)(2,1)} %refs_1_.1), custom_call_target="tpu_custom_call" | custom-call | tf_op jit(solution)/shard_map/emb_gather/pallas_call | solution.py:230
  60.8 8.5 %collective-permute-done.10 = bf16[384,768]{1,0:T(8,128)(2,1)} collective-permute-done((bf16[384,768]{1,0:T(8,128)(2,1)}, bf16[384,768]{1,0:T(8,128)(2,1)}, u32[]{:S(2)}, u32[]{:S(2)}) %collective-permute-start.10) | collective-permute-done | bytes 589856 | tf_op jit(solution)/shard_map/ppermute | solution.py:24
  69.8 11.5 %collective-permute-done.13 = bf16[384,768]{1,0:T(8,128)(2,1)} collective-permute-done((bf16[384,768]{1,0:T(8,128)(2,1)}, bf16[384,768]{1,0:T(8,128)(2,1)}, u32[]{:S(2)}, u32[]{:S(2)}) %collective-permute-start.13) | collective-permute-done | bytes 589856 | tf_op jit(solution)/shard_map/ppermute | solution.py:24
  90.0 12.0 %collective-permute-done.8 = bf16[8,64,768]{2,1,0:T(8,128)(2,1)} collective-permute-done((bf16[8,64,768]{2,1,0:T(8,128)(2,1)}, bf16[8,64,768]{2,1,0:T(8,128)(2,1)}, u32[]{:S(2)}, u32[]{:S(2)}) %collective-permute-start.8) | collective-permute-done | bytes 786464 | tf_op jit(solution)/shard_map/ppermute | solution.py:24
  102.7 13.6 %collective-permute-done.9 = bf16[8,64,768]{2,1,0:T(8,128)(2,1)} collective-permute-done((bf16[8,64,768]{2,1,0:T(8,128)(2,1)}, bf16[8,64,768]{2,1,0:T(8,128)(2,1)}, u32[]{:S(2)}, u32[]{:S(2)}) %collective-permute-start.9) | collective-permute-done | bytes 786464 | tf_op jit(solution)/shard_map/ppermute | solution.py:24
  124.7 7.9 %collective-permute-done.14 = bf16[384,768]{1,0:T(8,128)(2,1)S(1)} collective-permute-done((bf16[384,768]{1,0:T(8,128)(2,1)}, bf16[384,768]{1,0:T(8,128)(2,1)S(1)}, u32[]{:S(2)}, u32[]{:S(2)}) %collective-permute-start.14) | collective-permute-done | bytes 589856 | tf_op jit(solution)/shard_map/ppermute | solution.py:489
  134.0 4.1 slice_add_fusion.2
  141.7 5.4 convert_add_fusion
  154.9 20.8 %collective-permute-done.2 = bf16[1024,768]{1,0:T(8,128)(2,1)} collective-permute-done((bf16[1024,768]{1,0:T(8,128)(2,1)}, bf16[1024,768]{1,0:T(8,128)(2,1)}, u32[]{:S(2)}, u32[]{:S(2)}) %collective-permute-start.2) | collective-permute-done | bytes 1572896 | tf_op jit(solution)/shard_map/ppermute | solution.py:24
  179.1 6.4 multiply_convert_fusion.1
  185.5 10.4 %attn_fwd.2 = bf16[4,4,64,768]{3,2,1,0:T(8,128)(2,1)} custom-call(f32[8,256,256]{2,1,0:T(8,128)} %get-tuple-element.113.mask_ref, bf16[4,4,64,2304]{3,2,1,0:T(8,128)(2,1)} %bitcast.206), custom_call_target="tpu_custom_call" | custom-call | flops 1610612736 | bytes 7077888 | tf_op jit(solution)/shard_map/attn_fwd/pallas_call | solution.py:138
  195.9 12.5 %collective-permute-done.6 = bf16[1024,768]{1,0:T(8,128)(2,1)} collective-permute-done((bf16[1024,768]{1,0:T(8,128)(2,1)}, bf16[1024,768]{1,0:T(8,128)(2,1)}, u32[]{:S(2)}, u32[]{:S(2)}) %collective-permute-start.6) | collective-permute-done | bytes 1572896 | tf_op jit(solution)/shard_map/ppermute | solution.py:24
  212.0 6.0 multiply_convert_fusion
  218.0 10.4 %attn_fwd.3 = bf16[4,4,64,768]{3,2,1,0:T(8,128)(2,1)} custom-call(f32[8,256,256]{2,1,0:T(8,128)} %get-tuple-element.113.mask_ref, bf16[4,4,64,2304]{3,2,1,0:T(8,128)(2,1)} %bitcast.204), custom_call_target="tpu_custom_call" | custom-call | flops 1610612736 | bytes 7077888 | tf_op jit(solution)/shard_map/attn_fwd/pallas_call | solution.py:138
  228.4 57.3 %shard_map.280 = (bf16[2048,768]{1,0:T(8,128)(2,1)}, bf16[2048,768]{1,0:T(8,128)(2,1)}, bf16[2048,768]{1,0:T(8,128)(2,1)}, bf16[2048,1536]{1,0:T(8,128)(2,1)}, b...) custom-call(bf16[1024,768]{1,0:T(8,128)(2,1)} %copy-done.5, ...), custom_call_target="tpu_custom_call" | custom-call | flops 41070624768 | bytes 100000000 | tf_op jit(solution)/shard_map/pallas_call | solution.py:456
  285.7 40.6 %shard_map.281 = (bf16[2048,768]{1,0:T(8,128)(2,1)}, bf16[2048,768]{1,0:T(8,128)(2,1)}, f32[1536,768]{1,0:T(8,128)}, bf16[1536,768]{1,0:T(8,128)(2,1)}, f32[384,...) custom-call(bf16[1024,768]{1,0:T(8,128)(2,1)} %bitcast.228, bf16[1024,768]{1,0:T(8,128)(2,1)} %bitcast.230, ...), custom_call_target="tpu_custom_call" | custom-call | flops 24159191040 | bytes 100000000 | tf_op jit(solution)/shard_map/pallas_call | solution.py:456
  326.3 22.8 %attn_bwd.2 = (bf16[4,4,64,2304]{3,2,1,0:T(8,128)(2,1)}, f32[8,2304]{1,0:T(8,128)}) custom-call(f32[8,256,256]{2,1,0:T(8,128)} %get-tuple-element.112.refs_0_, bf16[4,4,64,2304]{3,2,1,0:T(8,128)(2,1)} %bitcast.207, bf16[2,4,4,64,768]{4,3,2,1,0:T(8,128)(2,1)} %bitcast.273), custom_call_target="tpu_custom_call" | custom-call | flops 4026531840 | bytes 14155776 | tf_op jit(solution)/shard_map/attn_bwd/pallas_call | solution.py:150
  349.2 5.8 fusion.39
  355.0 4.4 fusion.32
  363.3 22.6 %attn_bwd.3 = (bf16[4,4,64,2304]{3,2,1,0:T(8,128)(2,1)}, f32[8,2304]{1,0:T(8,128)}) custom-call(f32[8,256,256]{2,1,0:T(8,128)} %get-tuple-element.112.refs_0_, bf16[4,4,64,2304]{3,2,1,0:T(8,128)(2,1)} %bitcast.205, bf16[2,4,4,64,768]{4,3,2,1,0:T(8,128)(2,1)} %bitcast.274), custom_call_target="tpu_custom_call" | custom-call | flops 4026531840 | bytes 14155776 | tf_op jit(solution)/shard_map/attn_bwd/pallas_call | solution.py:150
  385.9 9.0 %fusion.33 = (f32[768]{0:T(1024)S(1)}, f32[1024]{0:T(1024)S(1)}, f32[1024]{0:T(1024)S(1)}, f32[768]{0:T(1024)S(1)}, bf16[1024,768]{1,0:T(8,128)(2,1)}) fusion(bf16[1024,768]{1,0:T(8,128)(2,1)S(1)} %copy-done.4, f32[1024]{0:T(1024)S(1)} %add_rsqrt_fusion, f32[1024]{0:T(1024)S(1)} %broadcast_multiply_fusion.4, f32[768]{0:T(1024)S(1)} %convert_element_type.181, ...), kind=kOutput, calls=%fused_computation.55 | convolution fusion | flops 3633312256 | bytes 11428864 | tf_op jit(solution)/shard_map/dot_general | solution.py:34
  404.1 3.7 fusion.21.r_3_
  411.7 4.1 fusion.44
  420.7 16.0 %collective-permute-done.17 = bf16[8,64,768]{2,1,0:T(8,128)(2,1)S(1)} collective-permute-done((bf16[8,64,768]{2,1,0:T(8,128)(2,1)S(1)}, bf16[8,64,768]{2,1,0:T(8,128)(2,1)S(1)}, u32[]{:S(2)}, u32[]{:S(2)}) %collective-permute-start.17) | collective-permute-done | bytes 786464 | tf_op jit(solution)/shard_map/ppermute | solution.py:24
  437.5 14.2 %collective-permute-done.18 = bf16[8,64,768]{2,1,0:T(8,128)(2,1)S(1)} collective-permute-done((bf16[8,64,768]{2,1,0:T(8,128)(2,1)S(1)}, bf16[8,64,768]{2,1,0:T(8,128)(2,1)S(1)}, u32[]{:S(2)}, u32[]{:S(2)}) %collective-permute-start.18) | collective-permute-done | bytes 786464 | tf_op jit(solution)/shard_map/ppermute | solution.py:24
  453.2 25.2 %collective-permute-done.30 = bf16[1,192,768]{2,1,0:T(8,128)(2,1)S(1)} collective-permute-done((bf16[1,192,768]{2,1,0:T(8,128)(2,1)S(1)}, bf16[1,192,768]{2,1,0:T(8,128)(2,1)S(1)}, u32[]{:S(2)}, u32[]{:S(2)}) %collective-permute-start.30) | collective-permute-done | bytes 294944 | tf_op jit(solution)/shard_map/ppermute | solution.py:24
  486.9 4.8 convert_add_fusion.3
  492.9 19.3 %collective-permute-done.22.r_7_ = bf16[1024,768]{1,0:T(8,128)(2,1)} collective-permute-done((bf16[1024,768]{1,0:T(8,128)(2,1)}, bf16[1024,768]{1,0:T(8,128)(2,1)}, u32[]{:S(2)}, u32[]{:S(2)}) %collective-permute-start.22) | collective-permute-done | bytes 1572896 | tf_op jit(solution)/shard_map/ppermute | solution.py:24
  512.2 32.8 %collective-permute-done.21.r_6_ = bf16[1024,768]{1,0:T(8,128)(2,1)} collective-permute-done((bf16[1024,768]{1,0:T(8,128)(2,1)}, bf16[1024,768]{1,0:T(8,128)(2,1)}, u32[]{:S(2)}, u32[]{:S(2)}) %collective-permute-start.21) | collective-permute-done | bytes 1572896 | tf_op jit(solution)/shard_map/ppermute | solution.py:24
  558.3 16.2 %collective-permute-done.28 = bf16[3,192,768]{2,1,0:T(8,128)(2,1)S(1)} collective-permute-done((bf16[3,192,768]{2,1,0:T(8,128)(2,1)}, bf16[3,192,768]{2,1,0:T(8,128)(2,1)S(1)}, u32[]{:S(2)}, u32[]{:S(2)}) %collective-permute-start.28) | collective-permute-done | bytes 884768 | tf_op jit(solution)/shard_map/ppermute | solution.py:24
  577.9 54.6 %emb_scatter.1 = f32[1571,8,768]{2,1,0:T(8,128)} custom-call(s32[8192]{0:T(1024)} %fusion.101.r_0_, s32[512]{0:T(512)} %or_convert_fusion.r_1_, bf16[1024,768]{1,0:T(8,128)(2,1)} %fusion.28.r_2_, bf16[1024,768]{1,0:T(8,128)(2,1)} %fusion.21.r_3_, bf16[1024,768]{1,0:T(8,128)(2,1)} %collective-permute-done.19.r_4_, ...), custom_call_target="tpu_custom_call" | custom-call | flops 49999998976 | bytes 38608896 | tf_op jit(solution)/shard_map/emb_scatter/pallas_call | solution.py:338
  632.5 3.8 fusion.37
  (330 shorter events, 119.4 us)
Async XLA Ops:
  35.6 104.5 %collective-permute-start = (bf16[2048,768]{1,0:T(8,128)(2,1)}, bf16[2048,768]{1,0:T(8,128)(2,1)}, u32[]{:S(2)}, u32[]{:S(2)}) collective-permute-start(bf16[2048,768]{1,0:T(8,128)(2,1)} %get-tuple-element.44), channel_id=1, source_target_pairs={{0,1},{1,0},{2,3},{3,2},{4,5},{5,4},{6,7},{7,6}} | collective-permute-start | bytes 9437192 | tf_op jit(solution)/shard_map/ppermute | solution.py:24
  36.4 97.5 %collective-permute-start.1 = (bf16[2048,768]{1,0:T(8,128)(2,1)}, bf16[2048,768]{1,0:T(8,128)(2,1)}, u32[]{:S(2)}, u32[]{:S(2)}) collective-permute-start(bf16[2048,768]{1,0:T(8,128)(2,1)} %get-tuple-element.46), channel_id=1, source_target_pairs={{0,1},{1,0},{2,3},{3,2},{4,5},{5,4},{6,7},{7,6}} | collective-permute-start | bytes 9437192 | tf_op jit(solution)/shard_map/ppermute | solution.py:24
  38.7 18.0 %collective-permute-start.3 = (bf16[400,768]{1,0:T(8,128)(2,1)}, bf16[400,768]{1,0:T(8,128)(2,1)}, u32[]{:S(2)}, u32[]{:S(2)}) collective-permute-start(bf16[400,768]{1,0:T(8,128)(2,1)} %constant_dynamic-slice_fusion.3), channel_id=1, source_target_pairs={{0,2},{1,3},{2,0},{3,1},{4,6},{5,7},{6,4},{7,5}} | collective-permute-start | bytes 1843208 | tf_op jit(solution)/shard_map/ppermute | solution.py:24
  44.2 25.2 %collective-permute-start.10 = (bf16[384,768]{1,0:T(8,128)(2,1)}, bf16[384,768]{1,0:T(8,128)(2,1)}, u32[]{:S(2)}, u32[]{:S(2)}) collective-permute-start(bf16[384,768]{1,0:T(8,128)(2,1)} %dynamic-slice_bitcast_fusion.3), channel_id=1, source_target_pairs={{0,2},{1,3},{2,0},{3,1},{4,6},{5,7},{6,4},{7,5}} | collective-permute-start | bytes 1769480 | tf_op jit(solution)/shard_map/ppermute | solution.py:24
  45.1 36.2 %collective-permute-start.13 = (bf16[384,768]{1,0:T(8,128)(2,1)}, bf16[384,768]{1,0:T(8,128)(2,1)}, u32[]{:S(2)}, u32[]{:S(2)}) collective-permute-start(bf16[384,768]{1,0:T(8,128)(2,1)} %constant_dynamic-slice_fusion.1), channel_id=1, source_target_pairs={{0,2},{1,3},{2,0},{3,1},{4,6},{5,7},{6,4},{7,5}} | collective-permute-start | bytes 1769480 | tf_op jit(solution)/shard_map/ppermute | solution.py:24
  56.7 27.0 %collective-permute-start.4 = (bf16[400,768]{1,0:T(8,128)(2,1)}, bf16[400,768]{1,0:T(8,128)(2,1)}, u32[]{:S(2)}, u32[]{:S(2)}) collective-permute-start(bf16[400,768]{1,0:T(8,128)(2,1)} %collective-permute-done.3), channel_id=1, source_target_pairs={{0,4},{4,0},{1,5},{5,1},{2,6},{6,2},{3,7},{7,3}} | collective-permute-start | bytes 1843208 | tf_op jit(solution)/shard_map/ppermute | solution.py:489
  81.3 20.7 %collective-permute-start.8 = (bf16[8,64,768]{2,1,0:T(8,128)(2,1)}, bf16[8,64,768]{2,1,0:T(8,128)(2,1)}, u32[]{:S(2)}, u32[]{:S(2)}) collective-permute-start(bf16[8,64,768]{2,1,0:T(8,128)(2,1)} %get-tuple-element.100), channel_id=1, source_target_pairs={{0,2},{1,3},{2,0},{3,1},{4,6},{5,7},{6,4},{7,5}} | collective-permute-start | bytes 2359304 | tf_op jit(solution)/shard_map/ppermute | solution.py:24
  83.7 32.6 %collective-permute-start.9 = (bf16[8,64,768]{2,1,0:T(8,128)(2,1)}, bf16[8,64,768]{2,1,0:T(8,128)(2,1)}, u32[]{:S(2)}, u32[]{:S(2)}) collective-permute-start(bf16[8,64,768]{2,1,0:T(8,128)(2,1)} %get-tuple-element.99), channel_id=1, source_target_pairs={{0,3},{1,2},{2,1},{3,0},{4,7},{5,6},{6,5},{7,4}} | collective-permute-start | bytes 2359304 | tf_op jit(solution)/shard_map/ppermute | solution.py:24
  85.2 35.8 %collective-permute-start.11 = (bf16[384,768]{1,0:T(8,128)(2,1)}, bf16[384,768]{1,0:T(8,128)(2,1)}, u32[]{:S(2)}, u32[]{:S(2)}) collective-permute-start(bf16[384,768]{1,0:T(8,128)(2,1)} %collective-permute-done.10), channel_id=1, source_target_pairs={{0,4},{4,0},{1,5},{5,1},{2,6},{6,2},{3,7},{7,3}} | collective-permute-start | bytes 1769480 | tf_op jit(solution)/shard_map/ppermute | solution.py:489
  102.0 45.1 %collective-permute-start.5 = (bf16[2,800,768]{2,1,0:T(8,128)(2,1)}, bf16[2,800,768]{2,1,0:T(8,128)(2,1)}, u32[]{:S(2)}, u32[]{:S(2)}) collective-permute-start(bf16[2,800,768]{2,1,0:T(8,128)(2,1)} %get-tuple-element.102), channel_id=1, source_target_pairs={{0,1},{1,0},{2,3},{3,2},{4,5},{5,4},{6,7},{7,6}} | collective-permute-start | bytes 7372808 | tf_op jit(solution)/shard_map/ppermute | solution.py:24
  116.3 16.3 %collective-permute-start.14 = (bf16[384,768]{1,0:T(8,128)(2,1)}, bf16[384,768]{1,0:T(8,128)(2,1)S(1)}, u32[]{:S(2)}, u32[]{:S(2)}) collective-permute-start(bf16[384,768]{1,0:T(8,128)(2,1)} %collective-permute-done.13), channel_id=1, source_target_pairs={{0,4},{4,0},{1,5},{5,1},{2,6},{6,2},{3,7},{7,3}} | collective-permute-start | bytes 1769480 | tf_op jit(solution)/shard_map/ppermute | solution.py:489
  124.2 104.2 %collective-permute-start.12 = (bf16[2,768,768]{2,1,0:T(8,128)(2,1)}, bf16[2,768,768]{2,1,0:T(8,128)(2,1)}, u32[]{:S(2)}, u32[]{:S(2)}) collective-permute-start(bf16[2,768,768]{2,1,0:T(8,128)(2,1)} %pad_maximum_fusion.2), channel_id=1, source_target_pairs={{0,1},{1,0},{2,3},{3,2},{4,5},{5,4},{6,7},{7,6}} | collective-permute-start | bytes 7077896 | tf_op jit(solution)/shard_map/ppermute | solution.py:24
  138.1 37.6 %collective-permute-start.2 = (bf16[1024,768]{1,0:T(8,128)(2,1)}, bf16[1024,768]{1,0:T(8,128)(2,1)}, u32[]{:S(2)}, u32[]{:S(2)}) collective-permute-start(bf16[1024,768]{1,0:T(8,128)(2,1)} %get-tuple-element.93), channel_id=1, source_target_pairs={{0,2},{1,3},{2,0},{3,1},{4,6},{5,7},{6,4},{7,5}} | collective-permute-start | bytes 4718600 | tf_op jit(solution)/shard_map/ppermute | solution.py:24
  139.8 88.6 %collective-permute-start.15 = (bf16[2,768,768]{2,1,0:T(8,128)(2,1)}, bf16[2,768,768]{2,1,0:T(8,128)(2,1)}, u32[]{:S(2)}, u32[]{:S(2)}) collective-permute-start(bf16[2,768,768]{2,1,0:T(8,128)(2,1)} %pad_maximum_fusion.3), channel_id=1, source_target_pairs={{0,1},{1,0},{2,3},{3,2},{4,5},{5,4},{6,7},{7,6}} | collective-permute-start | bytes 7077896 | tf_op jit(solution)/shard_map/ppermute | solution.py:24
  140.0 68.4 %collective-permute-start.6 = (bf16[1024,768]{1,0:T(8,128)(2,1)}, bf16[1024,768]{1,0:T(8,128)(2,1)}, u32[]{:S(2)}, u32[]{:S(2)}) collective-permute-start(bf16[1024,768]{1,0:T(8,128)(2,1)} %get-tuple-element.92), channel_id=1, source_target_pairs={{0,2},{1,3},{2,0},{3,1},{4,6},{5,7},{6,4},{7,5}} | collective-permute-start | bytes 4718600 | tf_op jit(solution)/shard_map/ppermute | solution.py:24
  360.9 57.5 %collective-permute-start.29 = (bf16[384,768]{1,0:T(8,128)(2,1)}, bf16[384,768]{1,0:T(8,128)(2,1)}, u32[]{:S(2)}, u32[]{:S(2)}) collective-permute-start(bf16[384,768]{1,0:T(8,128)(2,1)} %get-tuple-element.66), channel_id=1, source_target_pairs={{0,1},{1,0},{2,3},{3,2},{4,5},{5,4},{6,7},{7,6}} | collective-permute-start | bytes 1769480 | tf_op jit(solution)/shard_map/ppermute | solution.py:24
  415.9 70.5 %collective-permute-start.27 = (bf16[1152,768]{1,0:T(8,128)(2,1)}, bf16[1152,768]{1,0:T(8,128)(2,1)}, u32[]{:S(2)}, u32[]{:S(2)}) collective-permute-start(bf16[1152,768]{1,0:T(8,128)(2,1)} %fusion.15), channel_id=1, source_target_pairs={{0,1},{1,0},{2,3},{3,2},{4,5},{5,4},{6,7},{7,6}} | collective-permute-start | bytes 5308424 | tf_op jit(solution)/shard_map/ppermute | solution.py:24
  416.4 20.4 %collective-permute-start.17 = (bf16[8,64,768]{2,1,0:T(8,128)(2,1)S(1)}, bf16[8,64,768]{2,1,0:T(8,128)(2,1)S(1)}, u32[]{:S(2)}, u32[]{:S(2)}) collective-permute-start(bf16[8,64,768]{2,1,0:T(8,128)(2,1)S(1)} %bitcast.237), channel_id=1, source_target_pairs={{0,2},{1,3},{2,0},{3,1},{4,6},{5,7},{6,4},{7,5}} | collective-permute-start | bytes 2359304 | tf_op jit(solution)/shard_map/ppermute | solution.py:24
  417.4 34.3 %collective-permute-start.18 = (bf16[8,64,768]{2,1,0:T(8,128)(2,1)S(1)}, bf16[8,64,768]{2,1,0:T(8,128)(2,1)S(1)}, u32[]{:S(2)}, u32[]{:S(2)}) collective-permute-start(bf16[8,64,768]{2,1,0:T(8,128)(2,1)S(1)} %bitcast.236), channel_id=1, source_target_pairs={{0,3},{1,2},{2,1},{3,0},{4,7},{5,6},{6,5},{7,4}} | collective-permute-start | bytes 2359304 | tf_op jit(solution)/shard_map/ppermute | solution.py:24
  418.4 60.6 %collective-permute-start.26 = (f32[280,768]{1,0:T(8,128)S(1)}, f32[280,768]{1,0:T(8,128)S(1)}, u32[]{:S(2)}, u32[]{:S(2)}) collective-permute-start(f32[280,768]{1,0:T(8,128)S(1)} %fusion.125), channel_id=1, source_target_pairs={{0,2},{1,3},{2,0},{3,1},{4,6},{5,7},{6,4},{7,5}} | collective-permute-start | bytes 2580488 | tf_op jit(solution)/shard_map/ppermute | solution.py:24
  420.2 124.7 %collective-permute-start.31 = (bf16[1536,768]{1,0:T(8,128)(2,1)}, bf16[1536,768]{1,0:T(8,128)(2,1)}, u32[]{:S(2)}, u32[]{:S(2)}) collective-permute-start(bf16[1536,768]{1,0:T(8,128)(2,1)} %get-tuple-element.68), channel_id=1, source_target_pairs={{0,1},{1,0},{2,3},{3,2},{4,5},{5,4},{6,7},{7,6}} | collective-permute-start | bytes 7077896 | tf_op jit(solution)/shard_map/ppermute | solution.py:24
  436.8 41.6 %collective-permute-start.30 = (bf16[1,192,768]{2,1,0:T(8,128)(2,1)S(1)}, bf16[1,192,768]{2,1,0:T(8,128)(2,1)S(1)}, u32[]{:S(2)}, u32[]{:S(2)}) collective-permute-start(bf16[1,192,768]{2,1,0:T(8,128)(2,1)S(1)} %fusion.62), channel_id=1, source_target_pairs={{0,2},{1,3},{2,0},{3,1},{4,6},{5,7},{6,4},{7,5}} | collective-permute-start | bytes 884744 | tf_op jit(solution)/shard_map/ppermute | solution.py:24
  451.8 60.4 %collective-permute-start.22 = (bf16[1024,768]{1,0:T(8,128)(2,1)}, bf16[1024,768]{1,0:T(8,128)(2,1)}, u32[]{:S(2)}, u32[]{:S(2)}) collective-permute-start(bf16[1024,768]{1,0:T(8,128)(2,1)} %fusion.21.r_3_), channel_id=1, source_target_pairs={{0,2},{1,3},{2,0},{3,1},{4,6},{5,7},{6,4},{7,5}} | collective-permute-start | bytes 4718600 | tf_op jit(solution)/shard_map/ppermute | solution.py:24
  478.4 66.6 %collective-permute-start.21 = (bf16[1024,768]{1,0:T(8,128)(2,1)}, bf16[1024,768]{1,0:T(8,128)(2,1)}, u32[]{:S(2)}, u32[]{:S(2)}) collective-permute-start(bf16[1024,768]{1,0:T(8,128)(2,1)} %fusion.28.r_2_), channel_id=1, source_target_pairs={{0,2},{1,3},{2,0},{3,1},{4,6},{5,7},{6,4},{7,5}} | collective-permute-start | bytes 4718600 | tf_op jit(solution)/shard_map/ppermute | solution.py:24
  479.0 73.7 %collective-permute-start.33 = (bf16[1536,768]{1,0:T(8,128)(2,1)}, bf16[1536,768]{1,0:T(8,128)(2,1)}, u32[]{:S(2)}, u32[]{:S(2)}) collective-permute-start(bf16[1536,768]{1,0:T(8,128)(2,1)} %get-tuple-element.70), channel_id=1, source_target_pairs={{0,1},{1,0},{2,3},{3,2},{4,5},{5,4},{6,7},{7,6}} | collective-permute-start | bytes 7077896 | tf_op jit(solution)/shard_map/ppermute | solution.py:24
  486.4 90.1 %collective-permute-start.20 = (bf16[1024,768]{1,0:T(8,128)(2,1)}, bf16[1024,768]{1,0:T(8,128)(2,1)}, u32[]{:S(2)}, u32[]{:S(2)}) collective-permute-start(bf16[1024,768]{1,0:T(8,128)(2,1)} %fusion.21.r_3_), channel_id=1, source_target_pairs={{0,1},{1,0},{2,3},{3,2},{4,5},{5,4},{6,7},{7,6}} | collective-permute-start | bytes 4718600 | tf_op jit(solution)/shard_map/ppermute | solution.py:24
  512.2 65.7 %collective-permute-start.19 = (bf16[1024,768]{1,0:T(8,128)(2,1)}, bf16[1024,768]{1,0:T(8,128)(2,1)}, u32[]{:S(2)}, u32[]{:S(2)}) collective-permute-start(bf16[1024,768]{1,0:T(8,128)(2,1)} %fusion.28.r_2_), channel_id=1, source_target_pairs={{0,1},{1,0},{2,3},{3,2},{4,5},{5,4},{6,7},{7,6}} | collective-permute-start | bytes 4718600 | tf_op jit(solution)/shard_map/ppermute | solution.py:24
  544.9 33.0 %collective-permute-start.24 = (bf16[1024,768]{1,0:T(8,128)(2,1)}, bf16[1024,768]{1,0:T(8,128)(2,1)}, u32[]{:S(2)}, u32[]{:S(2)}) collective-permute-start(bf16[1024,768]{1,0:T(8,128)(2,1)} %collective-permute-done.22.r_7_), channel_id=1, source_target_pairs={{0,1},{1,0},{2,3},{3,2},{4,5},{5,4},{6,7},{7,6}} | collective-permute-start | bytes 4718600 | tf_op jit(solution)/shard_map/ppermute | solution.py:24
  545.0 33.0 %collective-permute-start.23 = (bf16[1024,768]{1,0:T(8,128)(2,1)}, bf16[1024,768]{1,0:T(8,128)(2,1)}, u32[]{:S(2)}, u32[]{:S(2)}) collective-permute-start(bf16[1024,768]{1,0:T(8,128)(2,1)} %collective-permute-done.21.r_6_), channel_id=1, source_target_pairs={{0,1},{1,0},{2,3},{3,2},{4,5},{5,4},{6,7},{7,6}} | collective-permute-start | bytes 4718600 | tf_op jit(solution)/shard_map/ppermute | solution.py:24
  552.7 21.8 %collective-permute-start.28 = (bf16[3,192,768]{2,1,0:T(8,128)(2,1)}, bf16[3,192,768]{2,1,0:T(8,128)(2,1)S(1)}, u32[]{:S(2)}, u32[]{:S(2)}) collective-permute-start(bf16[3,192,768]{2,1,0:T(8,128)(2,1)} %fusion.56), channel_id=1, source_target_pairs={{0,2},{1,3},{2,0},{3,1},{4,6},{5,7},{6,4},{7,5}} | collective-permute-start | bytes 2654216 | tf_op jit(solution)/shard_map/ppermute | solution.py:24
  574.5 58.0 %collective-permute-start.34 = (bf16[1,768,768]{2,1,0:T(8,128)(2,1)}, bf16[1,768,768]{2,1,0:T(8,128)(2,1)}, u32[]{:S(2)}, u32[]{:S(2)}) collective-permute-start(bf16[1,768,768]{2,1,0:T(8,128)(2,1)} %fusion.55), channel_id=1, source_target_pairs={{0,2},{1,3},{2,0},{3,1},{4,6},{5,7},{6,4},{7,5}} | collective-permute-start | bytes 3538952 | tf_op jit(solution)/shard_map/ppermute | solution.py:24
  576.5 59.8 %collective-permute-start.32 = (bf16[1,768,768]{1,2,0:T(8,128)(2,1)S(1)}, bf16[1,768,768]{1,2,0:T(8,128)(2,1)}, u32[]{:S(2)}, u32[]{:S(2)}) collective-permute-start(bf16[1,768,768]{1,2,0:T(8,128)(2,1)S(1)} %bitcast.231), channel_id=1, source_target_pairs={{0,2},{1,3},{2,0},{3,1},{4,6},{5,7},{6,4},{7,5}} | collective-permute-start | bytes 3538952 | tf_op jit(solution)/shard_map/ppermute | solution.py:24
  (50 other events, 796.2 us)
